TPU v7x, 128 devices: a whole 4x4x4 slice. The times are simulated.
128 devices in a mesh: gx: 32 (over y, x_hi, z), gy: 4 (over x_lo, core).
Axes of the slice: x: 4 (x_hi: 2, x_lo: 2; x = x_hi * 2 + x_lo), y: 4, z: 4, core: 2. Of those that a mesh axis runs over, the one named last changes fastest.
Arguments:
- electric: float32 [3, 512, 512, 128], P(None, 'gx', 'gy'), may hold values from -6 to 6
- magnetic: float32 [3, 512, 512, 128], P(None, 'gx', 'gy'), may hold values from -6 to 6
- retention: float32 [512, 512, 128], P('gx', 'gy'), may hold values from 0.5 to 1
- coupling: float32 [512, 512, 128], P('gx', 'gy'), may hold values from 0.1 to 0.5
- spectrum_real: float32 [4, 4, 512, 512], P(None, None, 'gx', 'gy'), may hold values from -6 to 6
- spectrum_imag: float32 [4, 4, 512, 512], P(None, None, 'gx', 'gy'), may hold values from -6 to 6
- phases: float32 [4], replicated, may hold values from -3.140625 to 3.140625
Outputs:
- next_electric: float32 [3, 512, 512, 128], P(None, 'gx', 'gy')
- next_magnetic: float32 [3, 512, 512, 128], P(None, 'gx', 'gy')
- next_real: float32 [4, 4, 512, 512], P(None, None, 'gx', 'gy')
- next_imag: float32 [4, 4, 512, 512], P(None, None, 'gx', 'gy')
- far_field: float32 [2, 4, 4, 256, 256], P(None, None, None, 'gx', 'gy')
All inputs are finite; a program needn't handle non-finite values.
Results may differ from a plain program's by a relative error of at most 0.000071.
Values sent between devices are 32-bit elements; how exact they have to be, the bound alone decides.
A program may use at most 128 MiB of HBM per device.

v0:
```python
import math

import jax
import jax.numpy as jnp
from jax import lax
from jax.sharding import PartitionSpec as P

WAVES = 256
TOP_PLANE = 111


curl_step = 0.5


def passed_along(value, axis, by):
    devices = lax.axis_size(axis)
    pairs = [(i, i + by) for i in range(devices) if 0 <= i + by < devices]
    return lax.ppermute(value, axis, pairs)


def in_blocks(value, dim, devices):
    dims = value.shape
    blocks = value.reshape(*dims[:dim], devices, dims[dim] // devices, *dims[dim + 1 :])
    return jnp.moveaxis(blocks, dim, 0)


def sent_and_summed(value, axis, dim):
    devices = lax.axis_size(axis)
    blocks = lax.all_to_all(in_blocks(value, dim, devices), axis, 0, 0, tiled=True)
    return jnp.sum(blocks, axis=0)


def forward_diff(values, along):
    padded = jnp.pad(values, [(0, 1) if which == along else (0, 0) for which in range(values.ndim)])
    return lax.slice_in_dim(padded, 1, values.shape[along] + 1, axis=along) - values


def backward_diff(values, along):
    padded = jnp.pad(values, [(1, 0) if which == along else (0, 0) for which in range(values.ndim)])
    return values - lax.slice_in_dim(padded, 0, values.shape[along], axis=along)


def ahead_diff(values, border, along):
    upper = lax.slice_in_dim(values, 1, values.shape[along], axis=along)
    return jnp.concatenate([upper, border], axis=along) - values


def behind_diff(values, border, along):
    lower = lax.slice_in_dim(values, 0, values.shape[along] - 1, axis=along)
    return values - jnp.concatenate([border, lower], axis=along)


def tables(number, extent, offset):
    wave = 2 * jnp.arange(number, dtype=jnp.int32) + 1 - number
    places = offset + jnp.arange(extent, dtype=jnp.int32)
    folded = wave[:, None] * places[None, :] % (4 * number)
    angles = folded.astype(jnp.float32) * (math.pi / (2 * number))
    return (jnp.cos(angles), jnp.sin(angles))


def first_section(real_part, imag_part, cos_y, sin_y):
    highest = lax.Precision.HIGHEST
    part_real = jnp.einsum("cfxy,ky->cfxk", real_part, cos_y, precision=highest) + jnp.einsum(
        "cfxy,ky->cfxk", imag_part, sin_y, precision=highest
    )
    part_imag = jnp.einsum("cfxy,ky->cfxk", imag_part, cos_y, precision=highest) - jnp.einsum(
        "cfxy,ky->cfxk", real_part, sin_y, precision=highest
    )
    return (part_real, part_imag)


def second_section(part_real, part_imag, cos_x, sin_x):
    highest = lax.Precision.HIGHEST
    far_real = jnp.einsum("jx,cfxk->cfjk", cos_x, part_real, precision=highest) + jnp.einsum(
        "jx,cfxk->cfjk", sin_x, part_imag, precision=highest
    )
    far_imag = jnp.einsum("jx,cfxk->cfjk", cos_x, part_imag, precision=highest) - jnp.einsum(
        "jx,cfxk->cfjk", sin_x, part_real, precision=highest
    )
    return jnp.stack([far_real, far_imag])


def per_device(electric, magnetic, retention, coupling, spectrum_real, spectrum_imag, phases):
    elec_x, elec_y, elec_z = (electric[0], electric[1], electric[2])
    rows_elec = passed_along(electric[1:3, 0:1], "gx", -1)
    cols_elec = passed_along(electric[0:3:2, :, 0:1], "gy", -1)
    mag_x = magnetic[0] - curl_step * (
        ahead_diff(elec_z, cols_elec[1], 1) - forward_diff(elec_y, 2)
    )
    mag_y = magnetic[1] - curl_step * (
        forward_diff(elec_x, 2) - ahead_diff(elec_z, rows_elec[1], 0)
    )
    mag_z = magnetic[2] - curl_step * (
        ahead_diff(elec_y, rows_elec[0], 0) - ahead_diff(elec_x, cols_elec[0], 1)
    )
    next_magnetic = jnp.stack([mag_x, mag_y, mag_z])
    rows_magn = passed_along(next_magnetic[1:3, -1:], "gx", 1)
    cols_magn = passed_along(next_magnetic[0:3:2, :, -1:], "gy", 1)
    new_x = retention * elec_x + coupling * (
        behind_diff(mag_z, cols_magn[1], 1) - backward_diff(mag_y, 2)
    )
    new_y = retention * elec_y + coupling * (
        backward_diff(mag_x, 2) - behind_diff(mag_z, rows_magn[1], 0)
    )
    new_z = retention * elec_z + coupling * (
        behind_diff(mag_y, rows_magn[0], 0) - behind_diff(mag_x, cols_magn[0], 1)
    )
    next_electric = jnp.stack([new_x, new_y, new_z])
    tangent = jnp.stack(
        [
            new_x[:, :, TOP_PLANE],
            new_y[:, :, TOP_PLANE],
            mag_x[:, :, TOP_PLANE],
            mag_y[:, :, TOP_PLANE],
        ]
    )
    next_real = spectrum_real + tangent[:, None] * jnp.cos(phases)[None, :, None, None]
    next_imag = spectrum_imag - tangent[:, None] * jnp.sin(phases)[None, :, None, None]
    local_rows = electric.shape[1]
    local_cols = electric.shape[2]
    scale = 1.0 / math.sqrt(local_rows * lax.axis_size("gx") * local_cols * lax.axis_size("gy"))
    cos_y, sin_y = tables(WAVES, local_cols, lax.axis_index("gy") * local_cols)
    part_real, part_imag = first_section(next_real, next_imag, cos_y, sin_y)
    cos_full, sin_full = tables(WAVES, local_rows * lax.axis_size("gx"), 0)
    reduced = sent_and_summed(jnp.stack([part_real, part_imag]), "gy", 4)
    columns = lax.all_to_all(reduced, "gx", split_axis=4, concat_axis=3, tiled=True)
    finished = second_section(columns[0], columns[1], cos_full, sin_full)
    whole = lax.all_to_all(finished, "gx", split_axis=3, concat_axis=4, tiled=True)
    far_field = whole * scale
    return (next_electric, next_magnetic, next_real, next_imag, far_field)


def solution(mesh):
    placed = (
        P(None, "gx", "gy", None),
        P(None, "gx", "gy", None),
        P("gx", "gy", None),
        P("gx", "gy", None),
        P(None, None, "gx", "gy"),
        P(None, None, "gx", "gy"),
        P(),
    )
    return jax.shard_map(
        per_device,
        mesh=mesh,
        in_specs=placed,
        out_specs=(
            P(None, "gx", "gy", None),
            P(None, "gx", "gy", None),
            P(None, None, "gx", "gy"),
            P(None, None, "gx", "gy"),
            P(None, None, None, "gx", "gy"),
        ),
        check_vma=False,
    )
```

profile of v0, /device:TPU:0, one launch (start us, length us, event | category | flops | bytes accessed | tf_op | source)
XLA Modules:
  0.0 127.0 jit_solution(17802811058515703602)
XLA Ops:
  0.6 0.9 slice.123
  1.6 1.3 %collective-permute-start = (f32[2,1,128,128]{3,2,1,0:T(8,128)S(1)}, f32[2,1,128,128]{3,2,1,0:T(8,128)S(1)}, u32[]{:S(2)}, u32[]{:S(2)}) collective-permute-start(f32[2,1,128,128]{3,2,1,0:T(8,128)S(1)} %slice.123), channel_id=1, source_target_pairs={{4,0},{8,4},{12,8},{16,12},{20,16},{24,20},{28,24},{32,28},{36,32}... | collective-permute-start | bytes 393224 | tf_op jit(solution)/shard_map/ppermute | solution.py:18
  2.9 0.9 slice.127
  3.8 1.3 %collective-permute-start.1 = (f32[2,16,1,128]{3,1,2,0:T(8,128)S(1)}, f32[2,16,1,128]{3,1,2,0:T(8,128)S(1)}, u32[]{:S(2)}, u32[]{:S(2)}) collective-permute-start(f32[2,16,1,128]{3,1,2,0:T(8,128)S(1)} %bitcast.158), channel_id=1, source_target_pairs={{1,0},{2,1},{3,2},{5,4},{6,5},{7,6},{9,8},{10,9},{11,10},{13,12},{... | collective-permute-start | bytes 49160 | tf_op jit(solution)/shard_map/ppermute | solution.py:18
  5.1 1.3 %slice_bitcast_fusion.2 = f32[16,128,128]{2,1,0:T(8,128)S(1)} fusion(f32[3,16,128,128]{3,2,1,0:T(8,128)} %param.7), kind=kLoop, calls=%fused_computation.55 | loop fusion | bytes 2097152 | tf_op jit(solution)/shard_map/squeeze | solution.py:84
  6.4 3.7 %slice_bitcast_fusion.10 = (f32[15,128,128]{2,1,0:T(8,128)}, f32[1,15,128,128]{3,2,1,0:T(8,128)}, f32[15,128,128]{2,1,0:T(8,128)}) fusion(f32[3,16,128,128]{3,2,1,0:T(8,128)} %param.7), kind=kLoop, calls=%fused_computation.136 | loop fusion | bytes 4915200 | tf_op jit(solution)/shard_map/slice | solution.py:44
  10.1 1.6 %fusion.94 = (f32[16,127,128]{2,1,0:T(8,128)}, f32[1,16,127,128]{3,2,1,0:T(8,128)}) fusion(f32[16,128,128]{2,1,0:T(8,128)S(1)} %slice_bitcast_fusion.2), kind=kLoop, calls=%fused_computation.139 | loop fusion | bytes 3121152 | tf_op jit(solution)/shard_map/slice | solution.py:44
  11.9 2.5 %slice_bitcast_fusion = (f32[16,128,128]{2,1,0:T(8,128)S(1)}, f32[1,16,128,128]{3,2,1,0:T(8,128)S(1)}, f32[16,128,128]{2,1,0:T(8,128)S(1)}) fusion(f32[3,16,128,128]{3,2,1,0:T(8,128)S(1)} %copy-done, f32[1,16,1,128]{3,2,1,0:T(1,128)S(1)} %bitcast.151, f32[1,16,127,128]{3,2,1,0:T(8,128)} %get-tuple-element.60, f32[1,1,128,128]{3,2,1,0:T(8,128)S(1)} %get-tuple-element.65, ...), kind=kLoop, calls=%fused_computation.53 | loop fusion | flops 1835008 | bytes 9437184 | tf_op jit(solution)/shard_map/squeeze | solution.py:84
  14.4 0.1 slice.160
  14.5 0.4 copy-done.7
  15.0 0.3 copy-done.8
  15.2 0.3 copy-done.10
  15.5 0.3 copy-done.11
  15.8 1.8 %fusion.20 = (f32[16,128,128]{2,1,0:T(8,128)S(1)}, f32[16,128,128]{2,1,0:T(8,128)S(1)}, f32[16,128,128]{2,1,0:T(8,128)S(1)}) fusion(f32[1,128,128]{2,1,0:T(8,128)S(1)} %get-tuple-element.63, f32[15,128,128]{2,1,0:T(8,128)S(1)} %copy-done.10, f32[16,1,128]{2,1,0:T(1,128)S(1)} %bitcast.152, f32[16,127,128]{2,1,0:T(8,128)S(1)} %copy-done.8, ...), kind=kLoop, calls=%fused_computation.35 | loop fusion | flops 4980736 | bytes 15728640 | tf_op jit(solution)/shard_map/sub | solution.py:93
  17.6 1.2 slice_reduce_fusion
  18.8 0.2 pad_maximum_fusion
  19.0 3.3 %collective-permute-start.2 = (f32[2,16,1,128]{3,2,1,0:T(1,128)S(1)}, f32[2,16,1,128]{3,2,1,0:T(1,128)S(1)}, u32[]{:S(2)}, u32[]{:S(2)}) collective-permute-start(f32[2,16,1,128]{3,2,1,0:T(1,128)S(1)} %slice.139), channel_id=1, source_target_pairs={{0,1},{1,2},{2,3},{4,5},{5,6},{6,7},{8,9},{9,10},{10,11},{12,13},{... | collective-permute-start | bytes 49160 | tf_op jit(solution)/shard_map/ppermute | solution.py:18
  22.4 0.1 slice.168
  22.4 4.6 %collective-permute-start.3 = (f32[2,1,128,128]{3,2,1,0:T(8,128)S(1)}, f32[2,1,128,128]{3,2,1,0:T(8,128)S(1)}, u32[]{:S(2)}, u32[]{:S(2)}) collective-permute-start(f32[2,1,128,128]{3,2,1,0:T(8,128)S(1)} %pad_maximum_fusion.2), channel_id=1, source_target_pairs={{0,4},{4,8},{8,12},{12,16},{16,20},{20,24},{24,28},{28,32},{32,36}... | collective-permute-start | bytes 393224 | tf_op jit(solution)/shard_map/ppermute | solution.py:18
  27.0 0.1 slice.166
  27.1 3.5 %collective-permute-done.3 = f32[2,1,128,128]{3,2,1,0:T(8,128)S(1)} collective-permute-done((f32[2,1,128,128]{3,2,1,0:T(8,128)S(1)}, f32[2,1,128,128]{3,2,1,0:T(8,128)S(1)}, u32[]{:S(2)}, u32[]{:S(2)}) %collective-permute-start.3) | collective-permute-done | bytes 131104 | tf_op jit(solution)/shard_map/ppermute | solution.py:18
  30.7 2.6 %fusion.13 = (f32[16,128,128]{2,1,0:T(8,128)S(1)}, f32[1,16,128,128]{3,2,1,0:T(8,128)}, f32[16,128,128]{2,1,0:T(8,128)S(1)}) fusion(f32[16,128,128]{2,1,0:T(8,128)S(1)} %copy-done.13, f32[16,128,128]{2,1,0:T(8,128)S(1)} %get-tuple-element.49, f32[16,128,128]{2,1,0:T(8,128)S(1)} %get-tuple-element.48, f32[16,127,128]{2,1,0:T(8,128)S(1)} %bitcast.141, ...), kind=kLoop, calls=%fused_computation.23 | loop fusion | flops 5767168 | bytes 15728640 | tf_op jit(solution)/shard_map/add | solution.py:99
  33.4 1.0 copy-done.3
  34.3 1.2 slice_reduce_fusion.2
  35.5 0.1 multiply_subtract_fusion
  35.7 0.9 fusion.53
  36.6 0.9 fusion.51
  37.5 0.9 convolution_add_fusion
  38.5 0.2 stack.54
  38.8 0.9 convolution_subtract_fusion
  39.7 0.2 stack.55
  40.0 0.1 maximum_bitcast_fusion
  40.1 0.7 reshape.54
  40.8 11.2 %all_to_all.29 = f32[4,1,32768]{2,1,0:T(1,128)S(1)} all-to-all(f32[4,1,32768]{2,1,0:T(1,128)S(1)} %reshape.54), channel_id=1, replica_groups=mesh['gx'=32,'gy'=4] {'gy'}, dimensions={0} | all-to-all | bytes 1048576 | tf_op jit(solution)/shard_map/all_to_all | solution.py:29
  52.0 0.6 broadcast.103
  52.6 2.2 %reduce.8 = f32[4,32768]{1,0:T(4,128)S(1)} reduce(f32[4,1,32768]{2,1,0:T(1,128)S(1)} %all_to_all.29, f32[]{:T(128)} %broadcast.103), dimensions={1}, to_apply=%all_to_all.10.reduce_sub_computation | reduce | bytes 1048580 | tf_op jit(solution)/shard_map/all_to_all | solution.py:29
  54.8 0.5 reshape.55
  55.3 0.1 reduce_sum.9
  55.4 1.1 copy.231
  56.5 0.8 reshape.56
  57.4 26.5 %all_to_all.30 = f32[32,1,1024]{2,1,0:T(1,128)S(1)} all-to-all(f32[32,1,1024]{2,1,0:T(1,128)S(1)} %reshape.56), channel_id=1, replica_groups=mesh['gx'=32,'gy'=4] {'gx'}, dimensions={0} | all-to-all | bytes 262144 | tf_op jit(solution)/shard_map/all_to_all | solution.py:126
  83.9 1.0 reduce.9
  84.9 0.7 reshape.57
  85.6 0.6 copy.232
  86.2 0.1 fusion.93
  86.3 0.1 copy.248
  86.4 0.3 reshape.48
  86.7 2.8 %fusion.35 = f32[4,4,2,256]{3,1,2,0:T(4,128)S(1)} fusion(f32[4,4,512,2]{2,1,3,0:T(4,128)S(1)} %reshape.48, s32[256]{0:T(256)S(1)} %multiply_add_fusion.1), kind=kOutput, calls=%fused_computation.67 | convolution fusion | flops 52166656 | bytes 99328 | tf_op jit(solution)/shard_map/jx,cfxk->cfjk/dot_general | solution.py:74
  89.5 0.1 copy.249
  89.6 0.3 reshape.49
  89.9 2.8 %fusion.33 = f32[4,4,2,256]{3,1,2,0:T(4,128)S(1)} fusion(f32[4,4,512,2]{2,1,3,0:T(4,128)S(1)} %reshape.49, s32[256]{0:T(256)S(1)} %multiply_add_fusion.1), kind=kOutput, calls=%fused_computation.65 | convolution fusion | flops 52166656 | bytes 99328 | tf_op jit(solution)/shard_map/jx,cfxk->cfjk/dot_general | solution.py:77
  92.6 2.8 %fusion.1 = f32[1,4,4,256,2]{3,2,4,1,0:T(4,128)S(1)} fusion(f32[4,4,2,256]{3,1,2,0:T(4,128)S(1)} %fusion.35, f32[4,4,512,2]{2,1,3,0:T(4,128)S(1)} %reshape.49, s32[256]{0:T(256)S(1)} %multiply_add_fusion.1), kind=kOutput, calls=%fused_computation.11 | convolution fusion | flops 52174848 | bytes 132096 | tf_op jit(solution)/shard_map/jx,cfxk->cfjk/dot_general | solution.py:74
  95.5 2.8 %fusion = f32[1,4,4,256,2]{3,2,4,1,0:T(4,128)S(1)} fusion(f32[4,4,2,256]{3,1,2,0:T(4,128)S(1)} %fusion.33, f32[4,4,512,2]{2,1,3,0:T(4,128)S(1)} %reshape.48, s32[256]{0:T(256)S(1)} %multiply_add_fusion.1), kind=kOutput, calls=%fused_computation.9 | convolution fusion | flops 52174848 | bytes 132096 | tf_op jit(solution)/shard_map/jx,cfxk->cfjk/dot_general | solution.py:77
  98.3 2.3 %copy.239 = f32[2,4,4,256,2]{2,4,1,0,3:T(2,128)} copy(f32[2,4,4,256,2]{3,2,4,1,0:T(4,128)S(1)} %pad_maximum_fusion.3) | data formatting | bytes 131072 | tf_op jit(solution)/shard_map/stack | solution.py:80
  100.6 4.8 %reshape.58 = f32[32,1,512]{2,1,0:T(1,128)} reshape(f32[256,2,4,2,4]{4,3,2,1,0:T(2,128)} %bitcast.144) | data formatting | bytes 131072
  105.4 4.1 %all-to-all-start.2 = ((f32[32,1,512]{2,1,0:T(1,128)}), f32[32,1,512]{2,1,0:T(1,128)S(1)}, u32[]{:S(2)}, u32[]{:S(2)}) async-start(f32[32,1,512]{2,1,0:T(1,128)} %reshape.58), calls=%async_computation.2 | async-start | bytes 131072 | tf_op jit(solution)/shard_map/all_to_all | solution.py:128
  109.6 1.9 %pad_maximum_fusion.1 = f32[3,16,128,128]{3,2,1,0:T(8,128)} fusion(f32[1,16,128,128]{3,2,1,0:T(8,128)S(1)} %copy-done.9, f32[1,16,128,128]{3,2,1,0:T(8,128)S(1)} %bitcast.143, f32[1,16,128,128]{3,2,1,0:T(8,128)S(1)} %bitcast.142), kind=kLoop, calls=%fused_computation.1 | loop fusion | flops 1572864 | bytes 6291456 | tf_op jit(solution)/shard_map/stack | solution.py:108
  111.4 7.9 %all-to-all-done.2 = f32[32,1,512]{2,1,0:T(1,128)S(1)} async-done(((f32[32,1,512]{2,1,0:T(1,128)}), f32[32,1,512]{2,1,0:T(1,128)S(1)}, u32[]{:S(2)}, u32[]{:S(2)}) %all-to-all-start.2) | async-done | bytes 65568 | tf_op jit(solution)/shard_map/all_to_all | solution.py:128
  119.3 0.8 reduce.10
  120.1 3.2 %reshape.59 = f32[256,2,4,2,4]{4,3,2,1,0:T(2,128)S(1)} reshape(f32[32,512]{1,0:T(8,128)S(1)} %reduce.10) | data formatting | bytes 131072
  123.4 1.2 copy.240
  124.6 0.6 mul.179
  125.2 0.8 copy.242
  126.1 1.0 copy.243
  (53 shorter events, 0.4 us)
Async XLA Ops:
  1.6 10.2 %collective-permute-start = (f32[2,1,128,128]{3,2,1,0:T(8,128)S(1)}, f32[2,1,128,128]{3,2,1,0:T(8,128)S(1)}, u32[]{:S(2)}, u32[]{:S(2)}) collective-permute-start(f32[2,1,128,128]{3,2,1,0:T(8,128)S(1)} %slice.123), channel_id=1, source_target_pairs={{4,0},{8,4},{12,8},{16,12},{20,16},{24,20},{28,24},{32,28},{36,32}... | collective-permute-start | bytes 393224 | tf_op jit(solution)/shard_map/ppermute | solution.py:18
  3.8 8.0 %collective-permute-start.1 = (f32[2,16,1,128]{3,1,2,0:T(8,128)S(1)}, f32[2,16,1,128]{3,1,2,0:T(8,128)S(1)}, u32[]{:S(2)}, u32[]{:S(2)}) collective-permute-start(f32[2,16,1,128]{3,1,2,0:T(8,128)S(1)} %bitcast.158), channel_id=1, source_target_pairs={{1,0},{2,1},{3,2},{5,4},{6,5},{7,6},{9,8},{10,9},{11,10},{13,12},{... | collective-permute-start | bytes 49160 | tf_op jit(solution)/shard_map/ppermute | solution.py:18
  6.4 5.3 %copy-start.1 = (f32[16,128,128]{2,1,0:T(8,128)}, f32[16,128,128]{2,1,0:T(8,128)S(1)}, u32[]{:S(2)}) copy-start(f32[16,128,128]{2,1,0:T(8,128)S(1)} %slice_bitcast_fusion.2) | copy-start | bytes 3145732
  6.4 5.3 %copy-start.19 = (f32[4]{0:T(128)S(1)}, f32[4]{0:T(128)}, u32[]{:S(2)}) copy-start(f32[4]{0:T(128)} %param.13) | copy-start | bytes 52
  6.4 5.4 %copy-start = (f32[3,16,128,128]{3,2,1,0:T(8,128)S(1)}, f32[3,16,128,128]{3,2,1,0:T(8,128)}, u32[]{:S(2)}) copy-start(f32[3,16,128,128]{3,2,1,0:T(8,128)} %param.7) | copy-start | bytes 9437188
  11.8 2.7 %copy-start.2 = (f32[16,128,128]{2,1,0:T(8,128)S(1)}, f32[16,128,128]{2,1,0:T(8,128)}, u32[]{:S(2)}) copy-start(f32[16,128,128]{2,1,0:T(8,128)} %copy-done.1) | copy-start | bytes 3145732
  11.8 3.1 %copy-start.7 = (f32[3,16,128,128]{3,2,1,0:T(8,128)S(1)}, f32[3,16,128,128]{3,2,1,0:T(8,128)}, u32[]{:S(2)}) copy-start(f32[3,16,128,128]{3,2,1,0:T(8,128)} %param.8) | copy-start | bytes 9437188
  11.8 3.4 %copy-start.8 = (f32[16,127,128]{2,1,0:T(8,128)S(1)}, f32[16,127,128]{2,1,0:T(8,128)}, u32[]{:S(2)}) copy-start(f32[16,127,128]{2,1,0:T(8,128)} %get-tuple-element.59) | copy-start | bytes 3121156
  11.9 3.7 %copy-start.10 = (f32[15,128,128]{2,1,0:T(8,128)S(1)}, f32[15,128,128]{2,1,0:T(8,128)}, u32[]{:S(2)}) copy-start(f32[15,128,128]{2,1,0:T(8,128)} %get-tuple-element.51) | copy-start | bytes 2949124
  11.9 4.0 %copy-start.11 = (f32[15,128,128]{2,1,0:T(8,128)S(1)}, f32[15,128,128]{2,1,0:T(8,128)}, u32[]{:S(2)}) copy-start(f32[15,128,128]{2,1,0:T(8,128)} %get-tuple-element.53) | copy-start | bytes 2949124
  19.0 11.7 %copy-start.12 = (f32[3,16,128,128]{3,2,1,0:T(8,128)}, f32[3,16,128,128]{3,2,1,0:T(8,128)S(1)}, u32[]{:S(2)}) copy-start(f32[3,16,128,128]{3,2,1,0:T(8,128)S(1)} %pad_maximum_fusion) | copy-start | bytes 9437188
  19.0 11.7 %copy-start.13 = (f32[16,128,128]{2,1,0:T(8,128)S(1)}, f32[16,128,128]{2,1,0:T(8,128)}, u32[]{:S(2)}) copy-start(f32[16,128,128]{2,1,0:T(8,128)} %param.10) | copy-start | bytes 3145732
  19.0 11.7 %copy-start.14 = (f32[16,128,128]{2,1,0:T(8,128)S(1)}, f32[16,128,128]{2,1,0:T(8,128)}, u32[]{:S(2)}) copy-start(f32[16,128,128]{2,1,0:T(8,128)} %param.9) | copy-start | bytes 3145732
  19.0 8.1 %collective-permute-start.2 = (f32[2,16,1,128]{3,2,1,0:T(1,128)S(1)}, f32[2,16,1,128]{3,2,1,0:T(1,128)S(1)}, u32[]{:S(2)}, u32[]{:S(2)}) collective-permute-start(f32[2,16,1,128]{3,2,1,0:T(1,128)S(1)} %slice.139), channel_id=1, source_target_pairs={{0,1},{1,2},{2,3},{4,5},{5,6},{6,7},{8,9},{9,10},{10,11},{12,13},{... | collective-permute-start | bytes 49160 | tf_op jit(solution)/shard_map/ppermute | solution.py:18
  22.4 8.2 %collective-permute-start.3 = (f32[2,1,128,128]{3,2,1,0:T(8,128)S(1)}, f32[2,1,128,128]{3,2,1,0:T(8,128)S(1)}, u32[]{:S(2)}, u32[]{:S(2)}) collective-permute-start(f32[2,1,128,128]{3,2,1,0:T(8,128)S(1)} %pad_maximum_fusion.2), channel_id=1, source_target_pairs={{0,4},{4,8},{8,12},{12,16},{16,20},{20,24},{24,28},{28,32},{32,36}... | collective-permute-start | bytes 393224 | tf_op jit(solution)/shard_map/ppermute | solution.py:18
  30.7 4.8 %copy-start.17 = (f32[4,4,16,128]{3,2,1,0:T(8,128)S(1)}, f32[4,4,16,128]{3,2,1,0:T(8,128)}, u32[]{:S(2)}) copy-start(f32[4,4,16,128]{3,2,1,0:T(8,128)} %param.12) | copy-start | bytes 393220
  30.7 4.8 %copy-start.18 = (f32[4,4,16,128]{3,2,1,0:T(8,128)S(1)}, f32[4,4,16,128]{3,2,1,0:T(8,128)}, u32[]{:S(2)}) copy-start(f32[4,4,16,128]{3,2,1,0:T(8,128)} %param.11) | copy-start | bytes 393220
  33.4 1.0 copy-start.3
  33.4 2.1 %copy-start.5 = (f32[16,128,128]{2,1,0:T(8,128)}, f32[16,128,128]{2,1,0:T(8,128)S(1)}, u32[]{:S(2)}) copy-start(f32[16,128,128]{2,1,0:T(8,128)S(1)} %get-tuple-element.47) | copy-start | bytes 3145732
  35.6 4.4 %copy-start.15 = (f32[4,4,16,128]{3,2,1,0:T(8,128)}, f32[4,4,16,128]{3,2,1,0:T(8,128)S(1)}, u32[]{:S(2)}) copy-start(f32[4,4,16,128]{3,2,1,0:T(8,128)S(1)} %get-tuple-element.66) | copy-start | bytes 393220
  35.7 4.4 %copy-start.16 = (f32[4,4,16,128]{3,2,1,0:T(8,128)}, f32[4,4,16,128]{3,2,1,0:T(8,128)S(1)}, u32[]{:S(2)}) copy-start(f32[4,4,16,128]{3,2,1,0:T(8,128)S(1)} %get-tuple-element.67) | copy-start | bytes 393220
  95.5 14.1 %copy-start.4 = (f32[16,128,128]{2,1,0:T(8,128)S(1)}, f32[16,128,128]{2,1,0:T(8,128)}, u32[]{:S(2)}) copy-start(f32[16,128,128]{2,1,0:T(8,128)} %copy-done.3) | copy-start | bytes 3145732
  95.5 14.1 %copy-start.6 = (f32[16,128,128]{2,1,0:T(8,128)S(1)}, f32[16,128,128]{2,1,0:T(8,128)}, u32[]{:S(2)}) copy-start(f32[16,128,128]{2,1,0:T(8,128)} %copy-done.5) | copy-start | bytes 3145732
  95.5 14.1 %copy-start.9 = (f32[1,16,128,128]{3,2,1,0:T(8,128)S(1)}, f32[1,16,128,128]{3,2,1,0:T(8,128)}, u32[]{:S(2)}) copy-start(f32[1,16,128,128]{3,2,1,0:T(8,128)} %get-tuple-element.46) | copy-start | bytes 3145732
  105.4 13.9 %all-to-all-start.2 = ((f32[32,1,512]{2,1,0:T(1,128)}), f32[32,1,512]{2,1,0:T(1,128)S(1)}, u32[]{:S(2)}, u32[]{:S(2)}) async-start(f32[32,1,512]{2,1,0:T(1,128)} %reshape.58), calls=%async_computation.2 | async-start | bytes 131072 | tf_op jit(solution)/shard_map/all_to_all | solution.py:128
where the time goes:
time: 128 us; the launch traced here: 127 us
  blocking collectives  37.7 us (29%)
  local copies, waits for them, and re-layouts  33.8 us (26%)
  matrix products  14.8 us (12%)
  starting transfers between devices  14.5 us (11%)
  other arithmetic  13.4 us (10%)
  waiting for transfers between devices  11.4 us (9%)
  between operations  1.33 us (1%)
    all_to_all x1, blocking collectives, per_device(): lax.all_to_all(reduced, 'gx', split_axis=4, concat_axis=3, tiled=True)  26.5 us
    unnamed x47, local copies, waits for them, and re-layouts  14.1 us
    all_to_all x1, blocking collectives, sent_and_summed(): lax.all_to_all(in_blocks(value, dim, devices), axis, 0, 0, tiled=True)  11.2 us
    ppermute x4, starting transfers between devices, passed_along(): return lax.ppermute(value, axis, pairs)  10.4 us
    all_to_all x1, waiting for transfers between devices, per_device(): lax.all_to_all(finished, 'gx', split_axis=3, concat_axis=4, tiled=True)  7.87 us
    slice x3, local copies, waits for them, and re-layouts, ahead_diff(): upper = lax.slice_in_dim(values, 1, values.shape[along], axis=along)  5.36 us
    all_to_all x1, starting transfers between devices, per_device(): lax.all_to_all(finished, 'gx', split_axis=3, concat_axis=4, tiled=True)  4.08 us
    ppermute x4, waiting for transfers between devices, passed_along(): return lax.ppermute(value, axis, pairs)  3.52 us
  transfers between devices with their start and end apart: 5, of which 2 were waited for; matrix products, arithmetic and copies ran while one was open for 8% of the time, Pallas kernels for 0%

commit v1 on v0

v1 whole, which is shorter than its diff:
```python
import functools
import math

import jax
import jax.numpy as jnp
import numpy as np
from jax import lax
from jax.experimental import pallas as pl
from jax.experimental.pallas import tpu as pltpu
from jax.sharding import PartitionSpec as P

MESH = pl.DeviceIdType.MESH
WAVES = 256
PLANE = 111
GX, GY = 32, 4
F32, BF16 = jnp.float32, jnp.bfloat16


def split_np(table):
    high = table.astype(np.float32).astype(jnp.bfloat16)
    low = (table - high.astype(np.float64)).astype(np.float32).astype(jnp.bfloat16)
    return np.stack([high, low])


def angle_np(wave, place):
    return (np.multiply.outer(wave, place) % 1024) * (math.pi / 512)


@functools.cache
def tables():
    wave = 2 * np.arange(WAVES) - 255
    ang = angle_np(wave, np.arange(512)).reshape(256, 4, 128).transpose(1, 0, 2)
    tab_y = split_np(np.concatenate([np.cos(ang), np.sin(ang)], axis=2))
    ang = angle_np(2 * np.arange(32) - 255, 16 * np.arange(32))
    eye = np.eye(8)
    tab_w = split_np(np.concatenate([np.kron(np.cos(ang), eye), np.kron(np.sin(ang), eye)], axis=1))
    ang = np.repeat(angle_np(2 * np.arange(32) - 255, np.arange(16)), 8, axis=0)
    cos, sin = np.tile(np.cos(ang), (1, 8)), np.tile(np.sin(ang), (1, 8))
    sin[:, 64:] *= -1
    tab_t = np.stack([cos, sin]).astype(np.float32)
    ang = 2 * math.pi * (np.multiply.outer(np.arange(8), np.arange(16)) % 16) / 16
    eye = np.eye(4)
    blocks = [np.einsum("ai,fg->afgi", t, eye).reshape(32, 64) for t in (np.cos(ang), np.sin(ang))]
    tab_g = split_np(np.concatenate(blocks, axis=1) / 512.0)
    return tab_y, tab_w, tab_t, tab_g


def split(value):
    high = value.astype(BF16)
    return high, (value - high.astype(F32)).astype(BF16)


def dot_nt(a, b):
    return lax.dot_general(a, b, (((1,), (1,)), ((), ())), preferred_element_type=F32)


def dot_nn(a, b):
    return lax.dot_general(a, b, (((1,), (0,)), ((), ())), preferred_element_type=F32)


def plane_of(value, at):
    wide = jnp.broadcast_to(value[:, at : at + 1], (128, 128))
    rows = lax.broadcasted_iota(jnp.int32, (128, 128), 0)
    lanes = lax.broadcasted_iota(jnp.int32, (128, 128), 1)
    return jnp.sum(jnp.where(rows == lanes, wide, 0.0), axis=0, keepdims=True)


def step_kernel(
    e_hbm, h_hbm, r_hbm, c_hbm, sr_hbm, si_hbm, ph_ref, ty_hbm, tw_hbm, tt_hbm, tg_hbm,
    eo, ho, nr, ni, far,
    eb, hb, rb, cb, srv, siv, ty, tw, tt, tg,
    ye_s, yh_s, ye_l, yh_l, xe_l, xh_l, ce_l, pk_s, pk_l, t_s, t_l, al,
    bs, bl, cs, cl, rel, zz,
    ld_sem, yh_sem, pk_ss, pk_rs, a_ss, a_rs, t_ss, t_rs, x_sem, b_ss, b_rs, c_ss, c_rs,
):
    X = lax.axis_index("gx")
    Y = lax.axis_index("gy")
    xn, xp = lax.rem(X + 1, GX), lax.rem(X + GX - 1, GX)
    yn, yp = lax.rem(Y + 1, GY), lax.rem(Y + GY - 1, GY)
    has_xn, has_xp, has_yn, has_yp = X < GX - 1, X > 0, Y < GY - 1, Y > 0

    barrier = pltpu.get_barrier_semaphore()
    me = X * GY + Y

    def greet(d, carry):
        other = lax.rem(me + d, GX * GY)
        pl.semaphore_signal(barrier, inc=1, device_id=(other // GY, lax.rem(other, GY)), device_id_type=MESH)
        return carry

    lax.fori_loop(1, GX * GY, greet, 0)

    loads = []

    def load(src, dst):
        copy = pltpu.make_async_copy(src, dst, ld_sem.at[len(loads)])
        copy.start()
        loads.append(copy)
        return copy

    first = [load(e_hbm.at[i], eb.at[i]) for i in range(3)] + [load(h_hbm.at[i], hb.at[i]) for i in range(3)]
    first += [load(c_hbm, cb)]
    ret = load(r_hbm, rb)
    spec = [load(sr_hbm, srv), load(si_hbm, siv)]
    tabs = [load(ty_hbm, ty), load(tw_hbm, tw), load(tt_hbm, tt), load(tg_hbm, tg)]

    rows = lax.broadcasted_iota(jnp.int32, (128, 128), 0)
    lanes = lax.broadcasted_iota(jnp.int32, (128, 128), 1)
    row16 = lax.broadcasted_iota(jnp.int32, (16, 128), 0)
    lane16 = lax.broadcasted_iota(jnp.int32, (16, 128), 1)
    lane1 = lax.broadcasted_iota(jnp.int32, (1, 128), 1)

    def next_z(v, lane):
        return jnp.where(lane == 127, 0.0, pltpu.roll(v, 127, 1))

    def prev_z(v, lane):
        return jnp.where(lane == 0, 0.0, pltpu.roll(v, 1, 1))

    @pl.when(jnp.logical_not(has_xn))
    def _():
        xe_l[...] = jnp.zeros_like(xe_l)
        pk_l[2] = jnp.zeros_like(pk_l[2])

    @pl.when(jnp.logical_not(has_xp))
    def _():
        xh_l[...] = jnp.zeros_like(xh_l)
        pk_l[0] = jnp.zeros_like(pk_l[0])

    @pl.when(jnp.logical_not(has_yn))
    def _():
        ye_l[...] = jnp.zeros_like(ye_l)

    @pl.when(jnp.logical_not(has_yp))
    def _():
        yh_l[...] = jnp.zeros_like(yh_l)

    @pl.when(jnp.logical_not(jnp.logical_and(has_xn, has_yp)))
    def _():
        ce_l[...] = jnp.zeros_like(ce_l)

    for copy in first:
        copy.wait()
    ye_s[0] = eb[0, :, 0, :]
    ye_s[1] = eb[2, :, 0, :]
    ex, ey, ez = eb[0, :, 127, :], eb[1, :, 127, :], eb[2, :, 127, :]
    yh_s[0] = hb[0, :, 127, :] - 0.5 * (-ez - (next_z(ey, lane16) - ey))
    ey_up = jnp.where(row16 == 15, 0.0, pltpu.roll(ey, 15, 0))
    yh_s[1] = hb[2, :, 127, :] - 0.5 * (ey_up - ey + ex)

    ex15 = eb[0, 15]
    ex_up = jnp.where(rows == 127, 0.0, pltpu.roll(ex15, 127, 0))
    phz = hb[2, 15] - 0.5 * (-eb[1, 15] - (ex_up - ex15))
    pk_s[0:1] = plane_of(eb[1, 0], PLANE)
    pk_s[1:2] = plane_of(eb[2, 0], PLANE)
    pk_s[2:3] = plane_of(eb[2, 0], PLANE - 1)
    pk_s[3:4] = plane_of(phz, PLANE)
    pk_s[4:5] = plane_of(cb[0], PLANE)
    pk_s[5:6] = plane_of(cb[15], PLANE)
    pk_s[6:7] = plane_of(ex15, PLANE)
    pk_s[7:8] = jnp.zeros((1, 128), F32)
    pk_l[1, Y] = pk_s[...]
    for copy in spec:
        copy.wait()
    al[0, Y] = srv[Y]
    al[1, Y] = siv[Y]
    ret.wait()

    pl.semaphore_wait(barrier, GX * GY - 1)

    def remote(src, dst, ss, rs, x, y):
        return pltpu.make_async_remote_copy(
            src_ref=src, dst_ref=dst, send_sem=ss, recv_sem=rs, device_id=(x, y), device_id_type=MESH
        )

    ye = remote(ye_s, ye_l, yh_sem.at[0], yh_sem.at[1], X, yp)
    yh = remote(yh_s, yh_l, yh_sem.at[2], yh_sem.at[3], X, yn)
    pl.when(has_yp)(ye.start)
    pl.when(has_yn)(yh.start)

    def pack(dx, d):
        return remote(
            pk_s, pk_l.at[2 - dx, Y], pk_ss.at[dx, d], pk_rs.at[2 - dx, Y], (xp, X, xn)[dx], lax.rem(Y + d, GY)
        )

    for dx, ok in ((0, has_xp), (2, has_xn)):
        for d in range(GY):
            pl.when(ok)(pack(dx, d).start)
    for d in range(1, GY):
        pack(1, d).start()

    def spectrum(part, d):
        g = lax.rem(Y + d, GY)
        return remote((srv, siv)[part].at[g], al.at[part, Y], a_ss.at[part, d], a_rs.at[part, Y], X, g)

    for d in range(1, GY):
        for part in range(2):
            spectrum(part, d).start()

    corner = remote(eb.at[1, 0, pl.ds(120, 8)], ce_l, x_sem.at[0], x_sem.at[1], xp, yn)
    pl.when(jnp.logical_and(has_xp, has_yn))(corner.start)
    xe = remote(eb.at[pl.ds(1, 2), 0], xe_l, x_sem.at[2], x_sem.at[3], xp, Y)
    pl.when(has_xp)(xe.start)

    pl.when(has_yn)(ye.wait_recv)
    pl.when(has_yp)(yh.wait_recv)
    yh_l[0] = jnp.where(has_yp, yh_l[0] - 0.5 * ye_s[1], 0.0)
    yh_l[1] = jnp.where(has_yp, yh_l[1] + 0.5 * ye_s[0], 0.0)

    def row(x, edge_first, edge_last):
        ex, ey, ez = eb[0, x], eb[1, x], eb[2, x]
        exn = jnp.where(rows == 127, ye_l[0, pl.ds(x, 1), :], pltpu.roll(ex, 127, 0))
        ezn = jnp.where(rows == 127, ye_l[1, pl.ds(x, 1), :], pltpu.roll(ez, 127, 0))
        if edge_last:
            ey_x, ez_x = -ey, -ez
        else:
            ey_x, ez_x = eb[1, x + 1] - ey, eb[2, x + 1] - ez
        hx = hb[0, x] - 0.5 * ((ezn - ez) - (next_z(ey, lanes) - ey))
        hy = hb[1, x] - 0.5 * ((next_z(ex, lanes) - ex) - ez_x)
        hz = hb[2, x] - 0.5 * (ey_x - (exn - ex))
        ho[0, x] = hx
        ho[1, x] = hy
        ho[2, x] = hz
        hxp = jnp.where(rows == 0, yh_l[0, pl.ds(x, 1), :], pltpu.roll(hx, 1, 0))
        hzp = jnp.where(rows == 0, yh_l[1, pl.ds(x, 1), :], pltpu.roll(hz, 1, 0))
        if edge_first:
            hy_x, hz_x = hy, hz
        else:
            hy_x, hz_x = hy - ho[1, x - 1], hz - ho[2, x - 1]
        r, c = rb[x], cb[x]
        nx = r * ex + c * ((hz - hzp) - (hy - prev_z(hy, lanes)))
        ny = r * ey + c * ((hx - prev_z(hx, lanes)) - hz_x)
        nz = r * ez + c * (hy_x - (hx - hxp))
        eo[0, x] = nx
        eo[1, x] = ny
        eo[2, x] = nz
        for at, v in enumerate((nx, ny, hx, hy)):
            t_s[at, pl.ds(x, 1), :] = plane_of(v, PLANE)

    row(0, True, False)

    def inner(x, carry):
        row(x, False, False)
        return carry

    lax.fori_loop(1, 15, inner, 0)
    row(15, False, True)

    def tangent(d):
        g = lax.rem(Y + d, GY)
        return remote(t_s.at[g], t_l.at[Y], t_ss.at[d], t_rs.at[Y], X, g)

    for d in range(1, GY):
        tangent(d).start()
    t_l[Y] = t_s[Y]
    xh = remote(ho.at[pl.ds(1, 2), 15], xh_l, x_sem.at[4], x_sem.at[5], xn, Y)
    pl.when(has_xn)(xh.start)

    def from_gy(make, d):
        make(d).wait_recv()

    for d in range(1, GY):
        s = lax.rem(Y + d, GY)
        for part in range(2):
            remote(srv.at[0], al.at[part, s], a_ss.at[part, d], a_rs.at[part, s], X, s).wait_recv()
        remote(pk_s, pk_l.at[1, s], pk_ss.at[1, d], pk_rs.at[1, s], X, s).wait_recv()
        remote(t_s.at[0], t_l.at[s], t_ss.at[d], t_rs.at[s], X, s).wait_recv()
    for s in range(GY):
        pl.when(has_xn)(remote(pk_s, pk_l.at[2, s], pk_ss.at[2, s], pk_rs.at[2, s], xn, Y).wait_recv)
        pl.when(has_xp)(remote(pk_s, pk_l.at[0, s], pk_ss.at[0, s], pk_rs.at[0, s], xp, Y).wait_recv)
    for copy in tabs:
        copy.wait()

    wave_cos = [jnp.cos(jnp.full((8, 128), ph_ref[f], F32))[0:1] for f in range(4)]
    wave_sin = [jnp.sin(jnp.full((8, 128), ph_ref[f], F32))[0:1] for f in range(4)]
    total = None
    for s in range(GY):
        nxt, own, prv = pk_l[2, s], pk_l[1, s], pk_l[0, s]
        dhz = -0.5 * nxt[0:1]
        before = -0.5 * pk_l[2, s - 1][0:1, 127:128] if s else jnp.zeros((1, 1), F32)
        dhz_p = jnp.where(lane1 == 0, before, pltpu.roll(dhz, 1, 1))
        dhy = 0.5 * nxt[1:2]
        dhyd = dhy - 0.5 * nxt[2:3]
        after = 0.5 * pk_l[0, s + 1][6:7, 0:1] if s < GY - 1 else jnp.zeros((1, 1), F32)
        hzp = prv[3:4] - 0.5 * own[0:1] + jnp.where(lane1 == 127, after, 0.0)
        last = jnp.where(
            Y == 0, own[5:6] * (dhz - dhz_p - dhyd), jnp.where(Y == 1, -own[5:6] * dhz, jnp.where(Y == 3, dhy, 0.0))
        )
        head = jnp.where(jnp.logical_and(Y == 1, has_xp), own[4:5] * hzp, 0.0)
        t = t_l[s] + jnp.where(row16 == 15, last, 0.0) + jnp.where(row16 == 0, head, 0.0)
        re = jnp.concatenate([al[0, s, f] + t * wave_cos[f] for f in range(4)], axis=0)
        im = jnp.concatenate([al[1, s, f] - t * wave_sin[f] for f in range(4)], axis=0)
        data = jnp.concatenate(
            [jnp.concatenate([re, im], axis=0), jnp.concatenate([im, -re], axis=0)], axis=1
        )
        high, low = split(data)
        part = dot_nt(ty[0, s], high) + dot_nt(ty[0, s], low) + dot_nt(ty[1, s], high)
        total = part if total is None else total + part
    bs[...] = total.reshape(GX, 8, 128)

    def column(d):
        to = lax.rem(X + d, GX)
        return remote(bs.at[to], bl.at[X], b_ss.at[d], b_rs.at[X], to, Y)

    def b_start(d, carry):
        column(d).start()
        return carry

    lax.fori_loop(1, GX, b_start, 0)
    bl[X] = bs[X]

    pl.when(has_xn)(xe.wait_recv)
    pl.when(has_xp)(xh.wait_recv)
    pl.when(jnp.logical_and(has_xn, has_yp))(corner.wait_recv)
    pl.when(has_xn)(xh.wait_send)
    dhy, dhz = 0.5 * xe_l[1], -0.5 * xe_l[0]
    ho[1, 15] = ho[1, 15] + dhy
    ho[2, 15] = ho[2, 15] + dhz
    dhz_p = jnp.where(rows == 0, -0.5 * ce_l[7:8], pltpu.roll(dhz, 1, 0))
    c = cb[15]
    eo[0, 15] = eo[0, 15] + c * ((dhz - dhz_p) - (dhy - prev_z(dhy, lanes)))
    eo[1, 15] = eo[1, 15] - c * dhz
    eo[2, 15] = eo[2, 15] + c * dhy
    hyp = jnp.where(has_xp, xh_l[0] + 0.5 * eb[2, 0], 0.0)
    hzp = jnp.where(has_xp, xh_l[1] - 0.5 * eb[1, 0], 0.0)
    c = cb[0]
    eo[1, 0] = eo[1, 0] + c * hzp
    eo[2, 0] = eo[2, 0] - c * hyp
    for d in range(1, GY):
        tangent(d).wait_send()
    t_s[0, 15:16] = plane_of(eo[0, 15], PLANE)
    t_s[1, 15:16] = plane_of(eo[1, 15], PLANE)
    t_s[1, 0:1] = plane_of(eo[1, 0], PLANE)
    t_s[3, 15:16] = plane_of(ho[1, 15], PLANE)
    for at in range(4):
        t = t_s[at]
        for f in range(4):
            nr[at, f] = srv[at, f] + t * wave_cos[f]
            ni[at, f] = siv[at, f] - t * wave_sin[f]

    def b_wait(d, carry):
        src = lax.rem(X + d, GX)
        remote(bs.at[src], bl.at[src], b_ss.at[d], b_rs.at[src], src, Y).wait_recv()
        return carry

    lax.fori_loop(1, GX, b_wait, 0)

    block = bl[...].reshape(256, 128)
    sign = jnp.where(lax.broadcasted_iota(jnp.int32, (256, 128), 1) < 64, 1.0, -1.0)
    both = jnp.concatenate([block, pltpu.roll(block, 64, 1) * sign], axis=0)
    high, low = split(both)
    y = dot_nn(tw[0], high) + dot_nn(tw[0], low) + dot_nn(tw[1], high)
    y = y * tt[0] + pltpu.roll(y, 64, 1) * tt[1]
    y_sw = pltpu.roll(y, 64, 1) * sign
    pieces = []
    for b in range(4):
        pieces += [y[64 * b : 64 * b + 64], y_sw[64 * b : 64 * b + 64]]
    high, low = split(jnp.concatenate(pieces, axis=0))
    out = dot_nt(tg[0], high) + dot_nt(tg[0], low) + dot_nt(tg[1], high)
    for a in range(8):
        for b in range(4):
            cs[4 * a + b] = out[4 * a : 4 * a + 4, 128 * b : 128 * b + 128]

    home, slot = X // 8, lax.rem(X, 8)

    def finished(d):
        to = lax.rem(X + d, GX)
        return remote(cs.at[to], cl.at[Y, slot], c_ss.at[d], c_rs.at[Y, slot], to, home)

    def c_start(d, carry):
        pl.when(jnp.logical_or(d > 0, home != Y))(finished(d).start)
        return carry

    lax.fori_loop(0, GX, c_start, 0)

    @pl.when(home == Y)
    def _():
        cl[Y, slot] = cs[X]

    def c_wait(i, carry):
        g, q = i // 8, lax.rem(i, 8)
        src = 8 * Y + q

        @pl.when(jnp.logical_or(g != Y, src != X))
        def _():
            remote(cs.at[0], cl.at[g, q], c_ss.at[0], c_rs.at[g, q], src, g).wait_recv()

        return carry

    lax.fori_loop(0, 32, c_wait, 0)

    for q in range(8):
        for g in range(4):
            rel[q, 4 * g : 4 * g + 4, :] = cl[g, q]
    turned = [pltpu.roll(rel[q], 8 * q, 1) if q else rel[q] for q in range(8)]
    group = lane16 // 8
    for s in range(16):
        acc = turned[0]
        for q in range(1, 8):
            acc = jnp.where(group == (q + s) % 16, turned[q], acc)
        if s:
            acc = pltpu.roll(acc, 128 - 8 * s, 1)
        zz[:, s, :] = acc
    for g in range(4):
        for f in range(4):
            far[0, g, f] = zz[4 * g + f, 0:8, 0:64]
            far[1, g, f] = zz[4 * g + f, 8:16, 0:64]

    pl.when(has_yp)(ye.wait_send)
    pl.when(has_yn)(yh.wait_send)
    for dx, ok in ((0, has_xp), (2, has_xn)):
        for d in range(GY):
            pl.when(ok)(pack(dx, d).wait_send)
    for d in range(1, GY):
        pack(1, d).wait_send()
        for part in range(2):
            spectrum(part, d).wait_send()
    pl.when(jnp.logical_and(has_xp, has_yn))(corner.wait_send)
    pl.when(has_xp)(xe.wait_send)

    def b_sent(d, carry):
        column(d).wait_send()
        return carry

    lax.fori_loop(1, GX, b_sent, 0)

    def c_sent(d, carry):
        pl.when(jnp.logical_or(d > 0, home != Y))(finished(d).wait_send)
        return carry

    lax.fori_loop(0, GX, c_sent, 0)


def flush_kernel(*refs):
    ins, outs, sem = refs[:5], refs[5:10], refs[10]
    copies = []
    for at, (src, dst) in enumerate(zip(ins, outs)):
        if at < 2:
            copies += [(src.at[i], dst.at[i]) for i in range(3)]
        else:
            copies.append((src, dst))
    copies = [pltpu.make_async_copy(src, dst, sem.at[at]) for at, (src, dst) in enumerate(copies)]
    for copy in copies:
        copy.start()
    for copy in copies:
        copy.wait()


def per_device(electric, magnetic, retention, coupling, spectrum_real, spectrum_imag, phases):
    tab_y, tab_w, tab_t, tab_g = (jnp.asarray(t) for t in tables())
    vmem, dma = pltpu.VMEM, pltpu.SemaphoreType.DMA
    hbm = pl.BlockSpec(memory_space=pltpu.HBM)
    in_vmem = pl.BlockSpec(memory_space=pltpu.VMEM)
    shapes = [
        jax.ShapeDtypeStruct(electric.shape, F32),
        jax.ShapeDtypeStruct(magnetic.shape, F32),
        jax.ShapeDtypeStruct(spectrum_real.shape, F32),
        jax.ShapeDtypeStruct(spectrum_imag.shape, F32),
        jax.ShapeDtypeStruct((2, 4, 4, 8, 64), F32),
    ]
    held = pl.pallas_call(
        step_kernel,
        out_shape=shapes,
        in_specs=[hbm] * 6 + [pl.BlockSpec(memory_space=pltpu.SMEM)] + [hbm] * 4,
        out_specs=[in_vmem] * 5,
        scratch_shapes=[
            vmem(electric.shape, F32), vmem(magnetic.shape, F32), vmem(retention.shape, F32), vmem(coupling.shape, F32),
            vmem(spectrum_real.shape, F32), vmem(spectrum_imag.shape, F32),
            vmem(tab_y.shape, BF16), vmem(tab_w.shape, BF16), vmem(tab_t.shape, F32), vmem(tab_g.shape, BF16),
            vmem((2, 16, 128), F32), vmem((2, 16, 128), F32), vmem((2, 16, 128), F32), vmem((2, 16, 128), F32),
            vmem((2, 128, 128), F32), vmem((2, 128, 128), F32), vmem((8, 128), F32),
            vmem((8, 128), F32), vmem((3, 4, 8, 128), F32),
            vmem((4, 16, 128), F32), vmem((4, 16, 128), F32), vmem((2, 4, 4, 16, 128), F32),
            vmem((32, 8, 128), F32), vmem((32, 8, 128), F32), vmem((32, 4, 128), F32), vmem((4, 8, 4, 128), F32),
            vmem((8, 16, 128), F32), vmem((16, 16, 128), F32),
            dma((14,)), dma((4,)), dma((3, 4)), dma((3, 4)), dma((2, 4)), dma((2, 4)), dma((4,)), dma((4,)), dma((6,)),
            dma((32,)), dma((32,)), dma((32,)), dma((4, 8)),
        ],
        compiler_params=pltpu.CompilerParams(collective_id=0, has_side_effects=True, vmem_limit_bytes=40 * 2**20),
    )(electric, magnetic, retention, coupling, spectrum_real, spectrum_imag, phases, tab_y, tab_w, tab_t, tab_g)
    return pl.pallas_call(
        flush_kernel,
        out_shape=shapes,
        in_specs=[in_vmem] * 5,
        out_specs=[hbm] * 5,
        scratch_shapes=[dma((9,))],
        compiler_params=pltpu.CompilerParams(vmem_limit_bytes=16 * 2**20),
    )(*held)


def solution(mesh):
    placed = (
        P(None, "gx", "gy", None),
        P(None, "gx", "gy", None),
        P("gx", "gy", None),
        P("gx", "gy", None),
        P(None, None, "gx", "gy"),
        P(None, None, "gx", "gy"),
        P(),
    )
    return jax.shard_map(
        per_device,
        mesh=mesh,
        in_specs=placed,
        out_specs=(
            P(None, "gx", "gy", None),
            P(None, "gx", "gy", None),
            P(None, None, "gx", "gy"),
            P(None, None, "gx", "gy"),
            P(None, None, None, "gx", "gy"),
        ),
        check_vma=False,
    )
```

time: 128 us -> 52.4 us (0.41)
  the two profiles are of different devices: /device:TPU:0 before, /device:TPU:1 now
where the time goes in v1:
time: 52.4 us; the launch traced here: 52 us
  Pallas kernels  40.6 us (77%)
  local copies, waits for them, and re-layouts  10.7 us (20%)
  between operations  0.66 us (1%)
    pallas_call x1, Pallas kernels, per_device(): pl.pallas_call(step_kernel, out_shape=shapes, in_specs=[hbm] * 6 + [pl.Bl...  37.8 us
    unnamed x20, local copies, waits for them, and re-layouts  10.7 us
    pallas_call x1, Pallas kernels, per_device(): pl.pallas_call(flush_kernel, out_shape=shapes, in_specs=[in_vmem] * 5, ou...  2.83 us

profile of v1, /device:TPU:1, one launch (start us, length us, event | category | flops | bytes accessed | tf_op | source)
XLA Modules:
  0.0 52.0 jit_solution(6063618734079433110)
XLA Ops:
  0.6 0.0 copy-start
  0.6 1.9 %copy-done = f32[3,16,128,128]{3,2,1,0:T(8,128)S(1)} copy-done((f32[3,16,128,128]{3,2,1,0:T(8,128)S(1)}, f32[3,16,128,128]{3,2,1,0:T(8,128)}, u32[]{:S(2)}) %copy-start) | copy-done | bytes 3145752
  2.5 0.0 copy-start.1
  2.5 1.2 %copy-done.1 = f32[16,128,128]{2,1,0:T(8,128)S(1)} copy-done((f32[16,128,128]{2,1,0:T(8,128)S(1)}, f32[16,128,128]{2,1,0:T(8,128)}, u32[]{:S(2)}) %copy-start.1) | copy-done | bytes 1048600
  3.7 0.0 copy-start.2
  3.8 1.2 %copy-done.2 = f32[16,128,128]{2,1,0:T(8,128)S(1)} copy-done((f32[16,128,128]{2,1,0:T(8,128)S(1)}, f32[16,128,128]{2,1,0:T(8,128)}, u32[]{:S(2)}) %copy-start.2) | copy-done | bytes 1048600
  5.0 0.0 copy-start.3
  5.0 1.2 %copy-done.3 = bf16[2,4,256,256]{3,2,1,0:T(8,128)(2,1)S(1)} copy-done((bf16[2,4,256,256]{3,2,1,0:T(8,128)(2,1)S(1)}, bf16[2,4,256,256]{3,2,1,0:T(8,128)(2,1)}, u32[]{:S(2)}) %copy-start.3) | copy-done | bytes 1048600
  6.2 0.0 copy-start.4
  6.2 1.0 %copy-done.4 = bf16[2,256,512]{2,1,0:T(8,128)(2,1)S(1)} copy-done((bf16[2,256,512]{2,1,0:T(8,128)(2,1)S(1)}, bf16[2,256,512]{2,1,0:T(8,128)(2,1)}, u32[]{:S(2)}) %copy-start.4) | copy-done | bytes 524312
  7.2 0.0 copy-start.5
  7.2 0.9 %copy-done.5 = f32[2,256,128]{2,1,0:T(8,128)S(1)} copy-done((f32[2,256,128]{2,1,0:T(8,128)S(1)}, f32[2,256,128]{2,1,0:T(8,128)}, u32[]{:S(2)}) %copy-start.5) | copy-done | bytes 262168
  8.2 0.0 copy-start.6
  8.2 0.9 %copy-done.6 = f32[4,4,16,128]{3,2,1,0:T(8,128)S(1)} copy-done((f32[4,4,16,128]{3,2,1,0:T(8,128)S(1)}, f32[4,4,16,128]{3,2,1,0:T(8,128)}, u32[]{:S(2)}) %copy-start.6) | copy-done | bytes 131096
  9.1 0.0 copy-start.7
  9.1 0.9 %copy-done.7 = f32[4,4,16,128]{3,2,1,0:T(8,128)S(1)} copy-done((f32[4,4,16,128]{3,2,1,0:T(8,128)S(1)}, f32[4,4,16,128]{3,2,1,0:T(8,128)}, u32[]{:S(2)}) %copy-start.7) | copy-done | bytes 131096
  10.0 0.0 copy-start.8
  10.0 0.7 %copy-done.8 = bf16[2,32,128]{2,1,0:T(8,128)(2,1)S(1)} copy-done((bf16[2,32,128]{2,1,0:T(8,128)(2,1)S(1)}, bf16[2,32,128]{2,1,0:T(8,128)(2,1)}, u32[]{:S(2)}) %copy-start.8) | copy-done | bytes 16408
  10.7 0.0 copy-start.9
  10.7 0.7 %copy-done.9 = f32[4]{0:T(128)S(1)} copy-done((f32[4]{0:T(128)S(1)}, f32[4]{0:T(128)}, u32[]{:S(2)}) %copy-start.9) | copy-done | bytes 40
  11.4 37.8 %shard_map.146 = (f32[3,16,128,128]{3,2,1,0:T(8,128)S(1)}, f32[3,16,128,128]{3,2,1,0:T(8,128)S(1)}, f32[4,4,16,128]{3,2,1,0:T(8,128)S(1)}, f32[4,4,16,128]{3,2,1,0:T(8,128)S(1)}, f32[2,4,4,8,64]{4,3,2,1,0:T(8,128)S(1)}) custom-call(f32[3,16,128,128]{3,2,1,0:T(8,128)S(1)} %copy-done, f32[3,16,128,128]{3,2,1,0:T(8,128)} %h_hbm.1, ...), custom_call_target="tpu_custom_call" | custom-call | tf_op jit(solution)/shard_map/pallas_call | solution.py:459
  49.1 2.8 %shard_map.147 = (f32[3,16,128,128]{3,2,1,0:T(8,128)}, f32[3,16,128,128]{3,2,1,0:T(8,128)}, f32[4,4,16,128]{3,2,1,0:T(8,128)}, f32[4,4,16,128]{3,2,1,0:T(8,128)}, f32[2,4,4,8,64]{4,3,2,1,0:T(8,128)}) custom-call(f32[3,16,128,128]{3,2,1,0:T(8,128)S(1)} %get-tuple-element.10.refs_0_, f32[3,16,128,128]{3,2,1,0:T(8,128)S(1)} %get-tuple-element.11.refs_1_, ...), custom_call_target="tpu_custom_call" | custom-call | tf_op jit(solution)/shard_map/pallas_call | solution.py:479
Async XLA Ops:
  0.6 1.9 %copy-start = (f32[3,16,128,128]{3,2,1,0:T(8,128)S(1)}, f32[3,16,128,128]{3,2,1,0:T(8,128)}, u32[]{:S(2)}) copy-start(f32[3,16,128,128]{3,2,1,0:T(8,128)} %e_hbm.1) | copy-start | bytes 9437188
  2.5 1.2 %copy-start.1 = (f32[16,128,128]{2,1,0:T(8,128)S(1)}, f32[16,128,128]{2,1,0:T(8,128)}, u32[]{:S(2)}) copy-start(f32[16,128,128]{2,1,0:T(8,128)} %r_hbm.1) | copy-start | bytes 3145732
  3.7 1.2 %copy-start.2 = (f32[16,128,128]{2,1,0:T(8,128)S(1)}, f32[16,128,128]{2,1,0:T(8,128)}, u32[]{:S(2)}) copy-start(f32[16,128,128]{2,1,0:T(8,128)} %c_hbm.1) | copy-start | bytes 3145732
  5.0 1.2 %copy-start.3 = (bf16[2,4,256,256]{3,2,1,0:T(8,128)(2,1)S(1)}, bf16[2,4,256,256]{3,2,1,0:T(8,128)(2,1)}, u32[]{:S(2)}) copy-start(bf16[2,4,256,256]{3,2,1,0:T(8,128)(2,1)} %constant.8.clone.ty_hbm) | copy-start | bytes 3145732
  6.2 1.0 %copy-start.4 = (bf16[2,256,512]{2,1,0:T(8,128)(2,1)S(1)}, bf16[2,256,512]{2,1,0:T(8,128)(2,1)}, u32[]{:S(2)}) copy-start(bf16[2,256,512]{2,1,0:T(8,128)(2,1)} %constant.9.clone.tw_hbm) | copy-start | bytes 1572868
  7.2 0.9 %copy-start.5 = (f32[2,256,128]{2,1,0:T(8,128)S(1)}, f32[2,256,128]{2,1,0:T(8,128)}, u32[]{:S(2)}) copy-start(f32[2,256,128]{2,1,0:T(8,128)} %constant.10.clone.tt_hbm) | copy-start | bytes 786436
  8.2 0.9 %copy-start.6 = (f32[4,4,16,128]{3,2,1,0:T(8,128)S(1)}, f32[4,4,16,128]{3,2,1,0:T(8,128)}, u32[]{:S(2)}) copy-start(f32[4,4,16,128]{3,2,1,0:T(8,128)} %sr_hbm.1) | copy-start | bytes 393220
  9.1 0.9 %copy-start.7 = (f32[4,4,16,128]{3,2,1,0:T(8,128)S(1)}, f32[4,4,16,128]{3,2,1,0:T(8,128)}, u32[]{:S(2)}) copy-start(f32[4,4,16,128]{3,2,1,0:T(8,128)} %si_hbm.1) | copy-start | bytes 393220
  10.0 0.7 %copy-start.8 = (bf16[2,32,128]{2,1,0:T(8,128)(2,1)S(1)}, bf16[2,32,128]{2,1,0:T(8,128)(2,1)}, u32[]{:S(2)}) copy-start(bf16[2,32,128]{2,1,0:T(8,128)(2,1)} %constant.11.clone.tg_hbm) | copy-start | bytes 49156
  10.7 0.7 %copy-start.9 = (f32[4]{0:T(128)S(1)}, f32[4]{0:T(128)}, u32[]{:S(2)}) copy-start(f32[4]{0:T(128)} %ph_ref.1) | copy-start | bytes 52

commit v2 on v1

--- a/solution.py
+++ b/solution.py
@@ -456,6 +456,10 @@
         jax.ShapeDtypeStruct(spectrum_imag.shape, F32),
         jax.ShapeDtypeStruct((2, 4, 4, 8, 64), F32),
     ]
+    fixed = [
+        pltpu.with_memory_space_constraint(a, pltpu.HBM)
+        for a in (electric, magnetic, retention, coupling, spectrum_real, spectrum_imag, tab_y, tab_w, tab_t, tab_g)
+    ]
     held = pl.pallas_call(
         step_kernel,
         out_shape=shapes,
@@ -475,7 +479,7 @@
             dma((32,)), dma((32,)), dma((32,)), dma((4, 8)),
         ],
         compiler_params=pltpu.CompilerParams(collective_id=0, has_side_effects=True, vmem_limit_bytes=40 * 2**20),
-    )(electric, magnetic, retention, coupling, spectrum_real, spectrum_imag, phases, tab_y, tab_w, tab_t, tab_g)
+    )(*fixed[:6], pltpu.with_memory_space_constraint(phases, pltpu.HBM), *fixed[6:])
     return pl.pallas_call(
         flush_kernel,
         out_shape=shapes,

time: 52.4 us -> 41.3 us (0.79)
  local copies, waits for them, and re-layouts: 10.7 us -> 0 us
    unnamed x20 -> x0, local copies, waits for them, and re-layouts: 10.7 us -> none
where the time goes in v2:
time: 41.3 us; the launch traced here: 41.2 us
  Pallas kernels  40.5 us (98%)
  between operations  0.64 us (2%)
    pallas_call x1, Pallas kernels, per_device(): pl.pallas_call(step_kernel, out_shape=shapes, in_specs=[hbm] * 6 + [pl.Bl...  37.7 us
    pallas_call x1, Pallas kernels, per_device(): pl.pallas_call(flush_kernel, out_shape=shapes, in_specs=[in_vmem] * 5, ou...  2.83 us

profile of v2, /device:TPU:1, one launch (start us, length us, event | category | flops | bytes accessed | tf_op | source)
XLA Modules:
  0.0 41.2 jit_solution(6822053041312630044)
XLA Ops:
  0.6 37.7 %shard_map.146 = (f32[3,16,128,128]{3,2,1,0:T(8,128)S(1)}, f32[3,16,128,128]{3,2,1,0:T(8,128)S(1)}, f32[4,4,16,128]{3,2,1,0:T(8,128)S(1)}, f32[4,4,16,128]{3,2,1,0:T(8,128)S(1)}, f32[2,4,4,8,64]{4,3,2,1,0:T(8,128)S(1)}) custom-call(f32[3,16,128,128]{3,2,1,0:T(8,128)} %e_hbm.1, f32[3,16,128,128]{3,2,1,0:T(8,128)} %h_hbm.1, f32[16,128,128]{2,1,0:T(8,128)} %r_hbm.1, ...), custom_call_target="tpu_custom_call" | custom-call | tf_op jit(solution)/shard_map/pallas_call | solution.py:463
  38.4 2.8 %shard_map.147 = (f32[3,16,128,128]{3,2,1,0:T(8,128)}, f32[3,16,128,128]{3,2,1,0:T(8,128)}, f32[4,4,16,128]{3,2,1,0:T(8,128)}, f32[4,4,16,128]{3,2,1,0:T(8,128)}, f32[2,4,4,8,64]{4,3,2,1,0:T(8,128)}) custom-call(f32[3,16,128,128]{3,2,1,0:T(8,128)S(1)} %get-tuple-element.10.refs_0_, f32[3,16,128,128]{3,2,1,0:T(8,128)S(1)} %get-tuple-element.11.refs_1_, ...), custom_call_target="tpu_custom_call" | custom-call | tf_op jit(solution)/shard_map/pallas_call | solution.py:483

commit v3 on v2

--- a/solution.py
+++ b/solution.py
@@ -67,10 +67,10 @@
 
 def step_kernel(
     e_hbm, h_hbm, r_hbm, c_hbm, sr_hbm, si_hbm, ph_ref, ty_hbm, tw_hbm, tt_hbm, tg_hbm,
-    eo, ho, nr, ni, far,
+    eo, ho, nr, ni, rel,
     eb, hb, rb, cb, srv, siv, ty, tw, tt, tg,
     ye_s, yh_s, ye_l, yh_l, xe_l, xh_l, ce_l, pk_s, pk_l, t_s, t_l, al,
-    bs, bl, cs, cl, rel, zz,
+    bs, bl, cs, cl, xh_s, pp,
     ld_sem, yh_sem, pk_ss, pk_rs, a_ss, a_rs, t_ss, t_rs, x_sem, b_ss, b_rs, c_ss, c_rs,
 ):
     X = lax.axis_index("gx")
@@ -79,15 +79,29 @@
     yn, yp = lax.rem(Y + 1, GY), lax.rem(Y + GY - 1, GY)
     has_xn, has_xp, has_yn, has_yp = X < GX - 1, X > 0, Y < GY - 1, Y > 0
 
+    pending = []
     barrier = pltpu.get_barrier_semaphore()
-    me = X * GY + Y
-
-    def greet(d, carry):
-        other = lax.rem(me + d, GX * GY)
-        pl.semaphore_signal(barrier, inc=1, device_id=(other // GY, lax.rem(other, GY)), device_id_type=MESH)
-        return carry
-
-    lax.fori_loop(1, GX * GY, greet, 0)
+    home, slot = X // 8, lax.rem(X, 8)
+
+    def greet(x, y):
+        pl.semaphore_signal(barrier, inc=1, device_id=(x, y), device_id_type=MESH)
+
+    def greet_gx(d, carry):
+        greet(lax.rem(X + d, GX), Y)
+        return carry
+
+    def greet_home(q, carry):
+        src = 8 * Y + q
+        for d in range(1, GY):
+            greet(src, lax.rem(Y + d, GY))
+        return carry
+
+    for d in range(1, GY):
+        for x in (xp, X, xn):
+            greet(x, lax.rem(Y + d, GY))
+    lax.fori_loop(1, GX, greet_gx, 0)
+    lax.fori_loop(0, 8, greet_home, 0)
+    greeted = 3 * (GY - 1) + (GX - 1) + jnp.where(home != Y, GX, 0)
 
     loads = []
 
@@ -97,11 +111,18 @@
         loads.append(copy)
         return copy
 
-    first = [load(e_hbm.at[i], eb.at[i]) for i in range(3)] + [load(h_hbm.at[i], hb.at[i]) for i in range(3)]
-    first += [load(c_hbm, cb)]
-    ret = load(r_hbm, rb)
+    chunks = []
+    for at in range(4):
+        part = pl.ds(4 * at, 4)
+        chunks.append(
+            [
+                load(e_hbm.at[:, part], eb.at[:, part]),
+                load(h_hbm.at[:, part], hb.at[:, part]),
+                load(c_hbm.at[part], cb.at[part]),
+                load(r_hbm.at[part], rb.at[part]),
+            ]
+        )
     spec = [load(sr_hbm, srv), load(si_hbm, siv)]
-    tabs = [load(ty_hbm, ty), load(tw_hbm, tw), load(tt_hbm, tt), load(tg_hbm, tg)]
 
     rows = lax.broadcasted_iota(jnp.int32, (128, 128), 0)
     lanes = lax.broadcasted_iota(jnp.int32, (128, 128), 1)
@@ -137,8 +158,60 @@
     def _():
         ce_l[...] = jnp.zeros_like(ce_l)
 
-    for copy in first:
-        copy.wait()
+    picks = (
+        (eb, 0, (110, 111, 112)), (eb, 1, (110, 111, 112)), (eb, 2, (110, 111)),
+        (hb, 0, (110, 111)), (hb, 1, (110, 111)), (hb, 2, (111,)),
+    )
+
+    def pick(x, carry):
+        at = 0
+        for ref, which, planes in picks:
+            v = ref[which, x]
+            for z in planes:
+                pp[at, pl.ds(x, 1), :] = plane_of(v, z)
+                at += 1
+        for ref in (rb, cb):
+            pp[at, pl.ds(x, 1), :] = plane_of(ref[x], PLANE)
+            at += 1
+        return carry
+
+    for at in range(4):
+        for copy in chunks[at]:
+            copy.wait()
+        lax.fori_loop(4 * at, 4 * at + 4, pick, 0)
+    tabs = [load(ty_hbm, ty), load(tw_hbm, tw), load(tt_hbm, tt), load(tg_hbm, tg)]
+
+    ex0, ex1, ex2, ey0, ey1, ey2, ez0, ez1, hx0, hx1, hy0, hy1, hz1, r1, c1 = (pp[at] for at in range(15))
+
+    def next_x(v):
+        return jnp.where(row16 == 15, 0.0, pltpu.roll(v, 15, 0))
+
+    def prev_x(v):
+        return jnp.where(row16 == 0, 0.0, pltpu.roll(v, 1, 0))
+
+    phx1 = hx1 - 0.5 * ((next_z(ez1, lane16) - ez1) - (ey2 - ey1))
+    phx0 = hx0 - 0.5 * ((next_z(ez0, lane16) - ez0) - (ey1 - ey0))
+    phy1 = hy1 - 0.5 * ((ex2 - ex1) - (next_x(ez1) - ez1))
+    phy0 = hy0 - 0.5 * ((ex1 - ex0) - (next_x(ez0) - ez0))
+    phz1 = hz1 - 0.5 * ((next_x(ey1) - ey1) - (next_z(ex1, lane16) - ex1))
+    t_s[0, 0:16] = r1 * ex1 + c1 * ((phz1 - prev_z(phz1, lane16)) - (phy1 - phy0))
+    t_s[1, 0:16] = r1 * ey1 + c1 * ((phx1 - phx0) - (phz1 - prev_x(phz1)))
+    t_s[2, 0:16] = phx1
+    t_s[3, 0:16] = phy1
+    cols = jnp.zeros((16, 128), F32)
+    for at, (v, y) in enumerate(((ex1, 0), (ez1, 0), (ez0, 0), (c1, 0), (phz1, 127), (c1, 127))):
+        cols = jnp.where(lane16 == at, v[:, y : y + 1], cols)
+    for g in range(GY):
+        t_s[g, 16:32] = cols
+    pk_s[0:1] = ey1[0:1]
+    pk_s[1:2] = ez1[0:1]
+    pk_s[2:3] = ez0[0:1]
+    pk_s[3:4] = phz1[15:16]
+    pk_s[4:5] = c1[0:1]
+    pk_s[5:6] = c1[15:16]
+    pk_s[6:7] = ex1[15:16]
+    pk_s[7:8] = jnp.zeros((1, 128), F32)
+
     ye_s[0] = eb[0, :, 0, :]
     ye_s[1] = eb[2, :, 0, :]
     ex, ey, ez = eb[0, :, 127, :], eb[1, :, 127, :], eb[2, :, 127, :]
@@ -146,35 +219,19 @@
     ey_up = jnp.where(row16 == 15, 0.0, pltpu.roll(ey, 15, 0))
     yh_s[1] = hb[2, :, 127, :] - 0.5 * (ey_up - ey + ex)
 
-    ex15 = eb[0, 15]
-    ex_up = jnp.where(rows == 127, 0.0, pltpu.roll(ex15, 127, 0))
-    phz = hb[2, 15] - 0.5 * (-eb[1, 15] - (ex_up - ex15))
-    pk_s[0:1] = plane_of(eb[1, 0], PLANE)
-    pk_s[1:2] = plane_of(eb[2, 0], PLANE)
-    pk_s[2:3] = plane_of(eb[2, 0], PLANE - 1)
-    pk_s[3:4] = plane_of(phz, PLANE)
-    pk_s[4:5] = plane_of(cb[0], PLANE)
-    pk_s[5:6] = plane_of(cb[15], PLANE)
-    pk_s[6:7] = plane_of(ex15, PLANE)
-    pk_s[7:8] = jnp.zeros((1, 128), F32)
     pk_l[1, Y] = pk_s[...]
     for copy in spec:
         copy.wait()
     al[0, Y] = srv[Y]
     al[1, Y] = siv[Y]
-    ret.wait()
-
-    pl.semaphore_wait(barrier, GX * GY - 1)
+    t_l[Y] = t_s[Y]
+
+    pl.semaphore_wait(barrier, greeted)
 
     def remote(src, dst, ss, rs, x, y):
         return pltpu.make_async_remote_copy(
             src_ref=src, dst_ref=dst, send_sem=ss, recv_sem=rs, device_id=(x, y), device_id_type=MESH
         )
-
-    ye = remote(ye_s, ye_l, yh_sem.at[0], yh_sem.at[1], X, yp)
-    yh = remote(yh_s, yh_l, yh_sem.at[2], yh_sem.at[3], X, yn)
-    pl.when(has_yp)(ye.start)
-    pl.when(has_yn)(yh.start)
 
     def pack(dx, d):
         return remote(
@@ -187,6 +244,23 @@
     for d in range(1, GY):
         pack(1, d).start()
 
+    def packs_sent():
+        for dx, ok in ((0, has_xp), (2, has_xn)):
+            for d in range(GY):
+                pl.when(ok)(pack(dx, d).wait_send)
+        for d in range(1, GY):
+            pack(1, d).wait_send()
+
+    pending.append(packs_sent)
+
+    def tangent(d):
+        g = lax.rem(Y + d, GY)
+        return remote(t_s.at[g], t_l.at[Y], t_ss.at[d], t_rs.at[Y], X, g)
+
+    for d in range(1, GY):
+        tangent(d).start()
+        pending.append(tangent(d).wait_send)
+
     def spectrum(part, d):
         g = lax.rem(Y + d, GY)
         return remote((srv, siv)[part].at[g], al.at[part, Y], a_ss.at[part, d], a_rs.at[part, Y], X, g)
@@ -194,16 +268,107 @@
     for d in range(1, GY):
         for part in range(2):
             spectrum(part, d).start()
+            pending.append(spectrum(part, d).wait_send)
+
+    ye = remote(ye_s, ye_l, yh_sem.at[0], yh_sem.at[1], X, yp)
+    yh = remote(yh_s, yh_l, yh_sem.at[2], yh_sem.at[3], X, yn)
+    pl.when(has_yp)(ye.start)
+    pl.when(has_yn)(yh.start)
+    pending.append(lambda: pl.when(has_yp)(ye.wait_send))
+    pending.append(lambda: pl.when(has_yn)(yh.wait_send))
 
     corner = remote(eb.at[1, 0, pl.ds(120, 8)], ce_l, x_sem.at[0], x_sem.at[1], xp, yn)
     pl.when(jnp.logical_and(has_xp, has_yn))(corner.start)
+    pending.append(lambda: pl.when(jnp.logical_and(has_xp, has_yn))(corner.wait_send))
     xe = remote(eb.at[pl.ds(1, 2), 0], xe_l, x_sem.at[2], x_sem.at[3], xp, Y)
     pl.when(has_xp)(xe.start)
+    pending.append(lambda: pl.when(has_xp)(xe.wait_send))
 
     pl.when(has_yn)(ye.wait_recv)
     pl.when(has_yp)(yh.wait_recv)
     yh_l[0] = jnp.where(has_yp, yh_l[0] - 0.5 * ye_s[1], 0.0)
     yh_l[1] = jnp.where(has_yp, yh_l[1] + 0.5 * ye_s[0], 0.0)
+
+    ex, ey, ez = eb[0, 15], eb[1, 15], eb[2, 15]
+    exn = jnp.where(rows == 127, ye_l[0, 15:16, :], pltpu.roll(ex, 127, 0))
+    xh_s[0] = hb[1, 15] - 0.5 * ((next_z(ex, lanes) - ex) + ez)
+    xh_s[1] = hb[2, 15] - 0.5 * (-ey - (exn - ex))
+    xh = remote(xh_s, xh_l, x_sem.at[4], x_sem.at[5], xn, Y)
+    pl.when(has_xn)(xh.start)
+    pending.append(lambda: pl.when(has_xn)(xh.wait_send))
+
+    def from_gy(make, d):
+        make(d).wait_recv()
+
+    for d in range(1, GY):
+        s = lax.rem(Y + d, GY)
+        for part in range(2):
+            remote(srv.at[0], al.at[part, s], a_ss.at[part, d], a_rs.at[part, s], X, s).wait_recv()
+        remote(pk_s, pk_l.at[1, s], pk_ss.at[1, d], pk_rs.at[1, s], X, s).wait_recv()
+        remote(t_s.at[0], t_l.at[s], t_ss.at[d], t_rs.at[s], X, s).wait_recv()
+    for s in range(GY):
+        pl.when(has_xn)(remote(pk_s, pk_l.at[2, s], pk_ss.at[2, s], pk_rs.at[2, s], xn, Y).wait_recv)
+        pl.when(has_xp)(remote(pk_s, pk_l.at[0, s], pk_ss.at[0, s], pk_rs.at[0, s], xp, Y).wait_recv)
+    for copy in tabs:
+        copy.wait()
+
+    wave_cos = [jnp.cos(jnp.full((8, 128), ph_ref[f], F32))[0:1] for f in range(4)]
+    wave_sin = [jnp.sin(jnp.full((8, 128), ph_ref[f], F32))[0:1] for f in range(4)]
+    total = None
+    for s in range(GY):
+        nxt, own, prv = pk_l[2, s], pk_l[1, s], pk_l[0, s]
+        dhz = -0.5 * nxt[0:1]
+        before = -0.5 * pk_l[2, s - 1][0:1, 127:128] if s else jnp.zeros((1, 1), F32)
+        dhz_p = jnp.where(lane1 == 0, before, pltpu.roll(dhz, 1, 1))
+        dhy = 0.5 * nxt[1:2]
+        dhyd = dhy - 0.5 * nxt[2:3]
+        after = 0.5 * pk_l[0, s + 1][6:7, 0:1] if s < GY - 1 else jnp.zeros((1, 1), F32)
+        hzp = prv[3:4] - 0.5 * own[0:1] + jnp.where(lane1 == 127, after, 0.0)
+        last = jnp.where(
+            Y == 0, own[5:6] * (dhz - dhz_p - dhyd), jnp.where(Y == 1, -own[5:6] * dhz, jnp.where(Y == 3, dhy, 0.0))
+        )
+        head = jnp.where(jnp.logical_and(Y == 1, has_xp), own[4:5] * hzp, 0.0)
+        t = t_l[s, 0:16] + jnp.where(row16 == 15, last, 0.0) + jnp.where(row16 == 0, head, 0.0)
+        mine = t_l[s, 16:32]
+        if s < GY - 1:
+            after = t_l[s + 1, 16:32]
+            exn, ez1n, ez0n, c127 = after[:, 0:1], after[:, 1:2], after[:, 2:3], mine[:, 5:6]
+            exn_p = prev_x(after)[:, 0:1]
+            edge = jnp.where(
+                Y == 0,
+                0.5 * c127 * exn,
+                jnp.where(Y == 1, -0.5 * c127 * ((ez1n - ez0n) + (exn - exn_p)), jnp.where(Y == 2, -0.5 * ez1n, 0.0)),
+            )
+            t = t + jnp.where(lane16 == 127, edge, 0.0)
+        if s > 0:
+            hzp0 = t_l[s - 1, 16:32][:, 4:5] + 0.5 * mine[:, 0:1]
+            t = t + jnp.where(lane16 == 0, jnp.where(Y == 0, -mine[:, 3:4] * hzp0, 0.0), 0.0)
+        re = jnp.concatenate([al[0, s, f] + t * wave_cos[f] for f in range(4)], axis=0)
+        im = jnp.concatenate([al[1, s, f] - t * wave_sin[f] for f in range(4)], axis=0)
+        data = jnp.concatenate(
+            [jnp.concatenate([re, im], axis=0), jnp.concatenate([im, -re], axis=0)], axis=1
+        )
+        high, low = split(data)
+        part = dot_nt(ty[0, s], high) + dot_nt(ty[0, s], low) + dot_nt(ty[1, s], high)
+        total = part if total is None else total + part
+    bs[...] = total.reshape(GX, 8, 128)
+
+    def column(d):
+        to = lax.rem(X + d, GX)
+        return remote(bs.at[to], bl.at[X], b_ss.at[d], b_rs.at[X], to, Y)
+
+    def b_start(d, carry):
+        column(d).start()
+        return carry
+
+    lax.fori_loop(1, GX, b_start, 0)
+
+    def b_sent(d, carry):
+        column(d).wait_send()
+        return carry
+
+    pending.append(lambda: lax.fori_loop(1, GX, b_sent, 0))
+    bl[X] = bs[X]
 
     def row(x, edge_first, edge_last):
         ex, ey, ez = eb[0, x], eb[1, x], eb[2, x]
@@ -232,9 +397,6 @@
         eo[0, x] = nx
         eo[1, x] = ny
         eo[2, x] = nz
-        for at, v in enumerate((nx, ny, hx, hy)):
-            t_s[at, pl.ds(x, 1), :] = plane_of(v, PLANE)
-
     row(0, True, False)
 
     def inner(x, carry):
@@ -243,74 +405,10 @@
 
     lax.fori_loop(1, 15, inner, 0)
     row(15, False, True)
-
-    def tangent(d):
-        g = lax.rem(Y + d, GY)
-        return remote(t_s.at[g], t_l.at[Y], t_ss.at[d], t_rs.at[Y], X, g)
-
-    for d in range(1, GY):
-        tangent(d).start()
-    t_l[Y] = t_s[Y]
-    xh = remote(ho.at[pl.ds(1, 2), 15], xh_l, x_sem.at[4], x_sem.at[5], xn, Y)
-    pl.when(has_xn)(xh.start)
-
-    def from_gy(make, d):
-        make(d).wait_recv()
-
-    for d in range(1, GY):
-        s = lax.rem(Y + d, GY)
-        for part in range(2):
-            remote(srv.at[0], al.at[part, s], a_ss.at[part, d], a_rs.at[part, s], X, s).wait_recv()
-        remote(pk_s, pk_l.at[1, s], pk_ss.at[1, d], pk_rs.at[1, s], X, s).wait_recv()
-        remote(t_s.at[0], t_l.at[s], t_ss.at[d], t_rs.at[s], X, s).wait_recv()
-    for s in range(GY):
-        pl.when(has_xn)(remote(pk_s, pk_l.at[2, s], pk_ss.at[2, s], pk_rs.at[2, s], xn, Y).wait_recv)
-        pl.when(has_xp)(remote(pk_s, pk_l.at[0, s], pk_ss.at[0, s], pk_rs.at[0, s], xp, Y).wait_recv)
-    for copy in tabs:
-        copy.wait()
-
-    wave_cos = [jnp.cos(jnp.full((8, 128), ph_ref[f], F32))[0:1] for f in range(4)]
-    wave_sin = [jnp.sin(jnp.full((8, 128), ph_ref[f], F32))[0:1] for f in range(4)]
-    total = None
-    for s in range(GY):
-        nxt, own, prv = pk_l[2, s], pk_l[1, s], pk_l[0, s]
-        dhz = -0.5 * nxt[0:1]
-        before = -0.5 * pk_l[2, s - 1][0:1, 127:128] if s else jnp.zeros((1, 1), F32)
-        dhz_p = jnp.where(lane1 == 0, before, pltpu.roll(dhz, 1, 1))
-        dhy = 0.5 * nxt[1:2]
-        dhyd = dhy - 0.5 * nxt[2:3]
-        after = 0.5 * pk_l[0, s + 1][6:7, 0:1] if s < GY - 1 else jnp.zeros((1, 1), F32)
-        hzp = prv[3:4] - 0.5 * own[0:1] + jnp.where(lane1 == 127, after, 0.0)
-        last = jnp.where(
-            Y == 0, own[5:6] * (dhz - dhz_p - dhyd), jnp.where(Y == 1, -own[5:6] * dhz, jnp.where(Y == 3, dhy, 0.0))
-        )
-        head = jnp.where(jnp.logical_and(Y == 1, has_xp), own[4:5] * hzp, 0.0)
-        t = t_l[s] + jnp.where(row16 == 15, last, 0.0) + jnp.where(row16 == 0, head, 0.0)
-        re = jnp.concatenate([al[0, s, f] + t * wave_cos[f] for f in range(4)], axis=0)
-        im = jnp.concatenate([al[1, s, f] - t * wave_sin[f] for f in range(4)], axis=0)
-        data = jnp.concatenate(
-            [jnp.concatenate([re, im], axis=0), jnp.concatenate([im, -re], axis=0)], axis=1
-        )
-        high, low = split(data)
-        part = dot_nt(ty[0, s], high) + dot_nt(ty[0, s], low) + dot_nt(ty[1, s], high)
-        total = part if total is None else total + part
-    bs[...] = total.reshape(GX, 8, 128)
-
-    def column(d):
-        to = lax.rem(X + d, GX)
-        return remote(bs.at[to], bl.at[X], b_ss.at[d], b_rs.at[X], to, Y)
-
-    def b_start(d, carry):
-        column(d).start()
-        return carry
-
-    lax.fori_loop(1, GX, b_start, 0)
-    bl[X] = bs[X]
 
     pl.when(has_xn)(xe.wait_recv)
     pl.when(has_xp)(xh.wait_recv)
     pl.when(jnp.logical_and(has_xn, has_yp))(corner.wait_recv)
-    pl.when(has_xn)(xh.wait_send)
     dhy, dhz = 0.5 * xe_l[1], -0.5 * xe_l[0]
     ho[1, 15] = ho[1, 15] + dhy
     ho[2, 15] = ho[2, 15] + dhz
@@ -324,18 +422,6 @@
     c = cb[0]
     eo[1, 0] = eo[1, 0] + c * hzp
     eo[2, 0] = eo[2, 0] - c * hyp
-    for d in range(1, GY):
-        tangent(d).wait_send()
-    t_s[0, 15:16] = plane_of(eo[0, 15], PLANE)
-    t_s[1, 15:16] = plane_of(eo[1, 15], PLANE)
-    t_s[1, 0:1] = plane_of(eo[1, 0], PLANE)
-    t_s[3, 15:16] = plane_of(ho[1, 15], PLANE)
-    for at in range(4):
-        t = t_s[at]
-        for f in range(4):
-            nr[at, f] = srv[at, f] + t * wave_cos[f]
-            ni[at, f] = siv[at, f] - t * wave_sin[f]
-
     def b_wait(d, carry):
         src = lax.rem(X + d, GX)
         remote(bs.at[src], bl.at[src], b_ss.at[d], b_rs.at[src], src, Y).wait_recv()
@@ -359,8 +445,6 @@
         for b in range(4):
             cs[4 * a + b] = out[4 * a : 4 * a + 4, 128 * b : 128 * b + 128]
 
-    home, slot = X // 8, lax.rem(X, 8)
-
     def finished(d):
         to = lax.rem(X + d, GX)
         return remote(cs.at[to], cl.at[Y, slot], c_ss.at[d], c_rs.at[Y, slot], to, home)
@@ -371,10 +455,28 @@
 
     lax.fori_loop(0, GX, c_start, 0)
 
+    def c_sent(d, carry):
+        pl.when(jnp.logical_or(d > 0, home != Y))(finished(d).wait_send)
+        return carry
+
+    pending.append(lambda: lax.fori_loop(0, GX, c_sent, 0))
+
     @pl.when(home == Y)
     def _():
         cl[Y, slot] = cs[X]
 
+    def own_plane(x, carry):
+        for at, v in enumerate((eo[0, x], eo[1, x], ho[0, x], ho[1, x])):
+            pp[at, pl.ds(x, 1), :] = plane_of(v, PLANE)
+        return carry
+
+    lax.fori_loop(0, 16, own_plane, 0)
+    for at in range(4):
+        t = pp[at]
+        for f in range(4):
+            nr[at, f] = srv[at, f] + t * wave_cos[f]
+            ni[at, f] = siv[at, f] - t * wave_sin[f]
+
     def c_wait(i, carry):
         g, q = i // 8, lax.rem(i, 8)
         src = 8 * Y + q
@@ -390,6 +492,17 @@
     for q in range(8):
         for g in range(4):
             rel[q, 4 * g : 4 * g + 4, :] = cl[g, q]
+    for wait in pending:
+        wait()
+
+
+def flush_kernel(eo, ho, nr, ni, rel, e_out, h_out, r_out, i_out, f_out, zz, fv, sem):
+    copies = [(eo.at[i], e_out.at[i]) for i in range(3)] + [(ho.at[i], h_out.at[i]) for i in range(3)]
+    copies += [(nr, r_out), (ni, i_out)]
+    copies = [pltpu.make_async_copy(src, dst, sem.at[at]) for at, (src, dst) in enumerate(copies)]
+    for copy in copies:
+        copy.start()
+    lane16 = lax.broadcasted_iota(jnp.int32, (16, 128), 1)
     turned = [pltpu.roll(rel[q], 8 * q, 1) if q else rel[q] for q in range(8)]
     group = lane16 // 8
     for s in range(16):
@@ -401,45 +514,10 @@
         zz[:, s, :] = acc
     for g in range(4):
         for f in range(4):
-            far[0, g, f] = zz[4 * g + f, 0:8, 0:64]
-            far[1, g, f] = zz[4 * g + f, 8:16, 0:64]
-
-    pl.when(has_yp)(ye.wait_send)
-    pl.when(has_yn)(yh.wait_send)
-    for dx, ok in ((0, has_xp), (2, has_xn)):
-        for d in range(GY):
-            pl.when(ok)(pack(dx, d).wait_send)
-    for d in range(1, GY):
-        pack(1, d).wait_send()
-        for part in range(2):
-            spectrum(part, d).wait_send()
-    pl.when(jnp.logical_and(has_xp, has_yn))(corner.wait_send)
-    pl.when(has_xp)(xe.wait_send)
-
-    def b_sent(d, carry):
-        column(d).wait_send()
-        return carry
-
-    lax.fori_loop(1, GX, b_sent, 0)
-
-    def c_sent(d, carry):
-        pl.when(jnp.logical_or(d > 0, home != Y))(finished(d).wait_send)
-        return carry
-
-    lax.fori_loop(0, GX, c_sent, 0)
-
-
-def flush_kernel(*refs):
-    ins, outs, sem = refs[:5], refs[5:10], refs[10]
-    copies = []
-    for at, (src, dst) in enumerate(zip(ins, outs)):
-        if at < 2:
-            copies += [(src.at[i], dst.at[i]) for i in range(3)]
-        else:
-            copies.append((src, dst))
-    copies = [pltpu.make_async_copy(src, dst, sem.at[at]) for at, (src, dst) in enumerate(copies)]
-    for copy in copies:
-        copy.start()
+            fv[0, g, f] = zz[4 * g + f, 0:8, 0:64]
+            fv[1, g, f] = zz[4 * g + f, 8:16, 0:64]
+    copies.append(pltpu.make_async_copy(fv, f_out, sem.at[8]))
+    copies[-1].start()
     for copy in copies:
         copy.wait()
 
@@ -462,7 +540,7 @@
     ]
     held = pl.pallas_call(
         step_kernel,
-        out_shape=shapes,
+        out_shape=shapes[:4] + [jax.ShapeDtypeStruct((8, 16, 128), F32)],
         in_specs=[hbm] * 6 + [pl.BlockSpec(memory_space=pltpu.SMEM)] + [hbm] * 4,
         out_specs=[in_vmem] * 5,
         scratch_shapes=[
@@ -472,10 +550,10 @@
             vmem((2, 16, 128), F32), vmem((2, 16, 128), F32), vmem((2, 16, 128), F32), vmem((2, 16, 128), F32),
             vmem((2, 128, 128), F32), vmem((2, 128, 128), F32), vmem((8, 128), F32),
             vmem((8, 128), F32), vmem((3, 4, 8, 128), F32),
-            vmem((4, 16, 128), F32), vmem((4, 16, 128), F32), vmem((2, 4, 4, 16, 128), F32),
+            vmem((4, 32, 128), F32), vmem((4, 32, 128), F32), vmem((2, 4, 4, 16, 128), F32),
             vmem((32, 8, 128), F32), vmem((32, 8, 128), F32), vmem((32, 4, 128), F32), vmem((4, 8, 4, 128), F32),
-            vmem((8, 16, 128), F32), vmem((16, 16, 128), F32),
-            dma((14,)), dma((4,)), dma((3, 4)), dma((3, 4)), dma((2, 4)), dma((2, 4)), dma((4,)), dma((4,)), dma((6,)),
+            vmem((2, 128, 128), F32), vmem((15, 16, 128), F32),
+            dma((22,)), dma((4,)), dma((3, 4)), dma((3, 4)), dma((2, 4)), dma((2, 4)), dma((4,)), dma((4,)), dma((6,)),
             dma((32,)), dma((32,)), dma((32,)), dma((4, 8)),
         ],
         compiler_params=pltpu.CompilerParams(collective_id=0, has_side_effects=True, vmem_limit_bytes=40 * 2**20),
@@ -485,7 +563,7 @@
         out_shape=shapes,
         in_specs=[in_vmem] * 5,
         out_specs=[hbm] * 5,
-        scratch_shapes=[dma((9,))],
+        scratch_shapes=[vmem((16, 16, 128), F32), vmem((2, 4, 4, 8, 64), F32), dma((9,))],
         compiler_params=pltpu.CompilerParams(vmem_limit_bytes=16 * 2**20),
     )(*held)
 

time: 41.3 us -> 39.6 us (0.959)
  Pallas kernels: 40.5 us -> 38.9 us
    pallas_call x1, Pallas kernels: 37.7 us -> 36 us  [per_device(): pl.pallas_call(step_kernel, out_shape=shapes[:4] + [jax.ShapeDtypeStruct(...]
where the time goes in v3:
time: 39.6 us; the launch traced here: 39.5 us
  Pallas kernels  38.9 us (98%)
  between operations  0.64 us (2%)
    pallas_call x1, Pallas kernels, per_device(): pl.pallas_call(step_kernel, out_shape=shapes[:4] + [jax.ShapeDtypeStruct(...  36 us
    pallas_call x1, Pallas kernels, per_device(): pl.pallas_call(flush_kernel, out_shape=shapes, in_specs=[in_vmem] * 5, ou...  2.93 us

profile of v3, /device:TPU:1, one launch (start us, length us, event | category | flops | bytes accessed | tf_op | source)
XLA Modules:
  0.0 39.5 jit_solution(18191772638946540011)
XLA Ops:
  0.6 36.0 %shard_map.146 = (f32[3,16,128,128]{3,2,1,0:T(8,128)S(1)}, f32[3,16,128,128]{3,2,1,0:T(8,128)S(1)}, f32[4,4,16,128]{3,2,1,0:T(8,128)S(1)}, f32[4,4,16,128]{3,2,1,0:T(8,128)S(1)}, f32[8,16,128]{2,1,0:T(8,128)S(1)}) custom-call(f32[3,16,128,128]{3,2,1,0:T(8,128)} %e_hbm.1, f32[3,16,128,128]{3,2,1,0:T(8,128)} %h_hbm.1, f32[16,128,128]{2,1,0:T(8,128)} %r_hbm.1, ...), custom_call_target="tpu_custom_call" | custom-call | tf_op jit(solution)/shard_map/pallas_call | solution.py:541
  36.6 2.9 %shard_map.147 = (f32[3,16,128,128]{3,2,1,0:T(8,128)}, f32[3,16,128,128]{3,2,1,0:T(8,128)}, f32[4,4,16,128]{3,2,1,0:T(8,128)}, f32[4,4,16,128]{3,2,1,0:T(8,128)}, f32[2,4,4,8,64]{4,3,2,1,0:T(8,128)}) custom-call(f32[3,16,128,128]{3,2,1,0:T(8,128)S(1)} %get-tuple-element.10.eo, f32[3,16,128,128]{3,2,1,0:T(8,128)S(1)} %get-tuple-element.11.ho, ...), custom_call_target="tpu_custom_call" | custom-call | tf_op jit(solution)/shard_map/pallas_call | solution.py:561

commit v4 on v3

--- a/solution.py
+++ b/solution.py
@@ -1,4 +1,5 @@
 import functools
+import itertools
 import math
 
 import jax
@@ -33,7 +34,9 @@
     tab_y = split_np(np.concatenate([np.cos(ang), np.sin(ang)], axis=2))
     ang = angle_np(2 * np.arange(32) - 255, 16 * np.arange(32))
     eye = np.eye(8)
-    tab_w = split_np(np.concatenate([np.kron(np.cos(ang), eye), np.kron(np.sin(ang), eye)], axis=1))
+    ang = ang.reshape(32, 4, 2, 4).transpose(2, 0, 1, 3).reshape(2, 32, 16)
+    tab_w = np.stack([np.concatenate([np.kron(np.cos(a), eye), np.kron(np.sin(a), eye)], axis=1) for a in ang])
+    tab_w = split_np(tab_w)
     ang = np.repeat(angle_np(2 * np.arange(32) - 255, np.arange(16)), 8, axis=0)
     cos, sin = np.tile(np.cos(ang), (1, 8)), np.tile(np.sin(ang), (1, 8))
     sin[:, 64:] *= -1
@@ -45,6 +48,10 @@
     return tab_y, tab_w, tab_t, tab_g
 
 
+def hops(o):
+    return min(o[0], 4 - o[0]) + 2 * o[1] + min(o[2], 4 - o[2])
+
+
 def split(value):
     high = value.astype(BF16)
     return high, (value - high.astype(F32)).astype(BF16)
@@ -66,12 +73,12 @@
 
 
 def step_kernel(
-    e_hbm, h_hbm, r_hbm, c_hbm, sr_hbm, si_hbm, ph_ref, ty_hbm, tw_hbm, tt_hbm, tg_hbm,
+    e_hbm, h_hbm, r_hbm, c_hbm, sr_hbm, si_hbm, ph_hbm, ty_hbm, tw_hbm, tt_hbm, tg_hbm,
     eo, ho, nr, ni, rel,
     eb, hb, rb, cb, srv, siv, ty, tw, tt, tg,
     ye_s, yh_s, ye_l, yh_l, xe_l, xh_l, ce_l, pk_s, pk_l, t_s, t_l, al,
-    bs, bl, cs, cl, xh_s, pp,
-    ld_sem, yh_sem, pk_ss, pk_rs, a_ss, a_rs, t_ss, t_rs, x_sem, b_ss, b_rs, c_ss, c_rs,
+    bs, bl, cs, cl, xh_s, pp, wv, ph_ref,
+    ld_sem, yh_sem, pk_ss, pk_rs, a_ss, a_rs, t_ss, t_rs, x_sem, b_ss, b_rs, c_ss, c_rs, ph_sem,
 ):
     X = lax.axis_index("gx")
     Y = lax.axis_index("gy")
@@ -82,25 +89,26 @@
     pending = []
     barrier = pltpu.get_barrier_semaphore()
     home, slot = X // 8, lax.rem(X, 8)
+    offsets = sorted(itertools.product(range(4), range(2), range(4)), key=lambda o: (-hops(o), o))
+    at_y = [((X // 8 + a) & 3) * 8 for a in range(4)]
+    at_x = [((X // 4 + b) & 1) * 4 for b in range(2)]
+    at_z = [(X + c) & 3 for c in range(4)]
+
+    def block_at(o):
+        return at_y[o[0]] + at_x[o[1]] + at_z[o[2]]
 
     def greet(x, y):
         pl.semaphore_signal(barrier, inc=1, device_id=(x, y), device_id_type=MESH)
 
-    def greet_gx(d, carry):
-        greet(lax.rem(X + d, GX), Y)
-        return carry
-
-    def greet_home(q, carry):
-        src = 8 * Y + q
-        for d in range(1, GY):
-            greet(src, lax.rem(Y + d, GY))
-        return carry
-
-    for d in range(1, GY):
-        for x in (xp, X, xn):
-            greet(x, lax.rem(Y + d, GY))
-    lax.fori_loop(1, GX, greet_gx, 0)
-    lax.fori_loop(0, 8, greet_home, 0)
+    others = [lax.rem(Y + d, GY) for d in range(1, GY)]
+    for o in offsets[:-1]:
+        greet(block_at(o), Y)
+    for x in (xp, xn, X):
+        for y in others:
+            greet(x, y)
+    for o in sorted(itertools.product(range(2), range(4)), key=lambda o: (-hops((0,) + o), o)):
+        for y in others:
+            greet(8 * Y + at_x[o[0]] + at_z[o[1]], y)
     greeted = 3 * (GY - 1) + (GX - 1) + jnp.where(home != Y, GX, 0)
 
     loads = []
@@ -111,6 +119,8 @@
         loads.append(copy)
         return copy
 
+    phase = pltpu.make_async_copy(ph_hbm, ph_ref, ph_sem)
+    phase.start()
     chunks = []
     for at in range(4):
         part = pl.ds(4 * at, 4)
@@ -123,6 +133,12 @@
             ]
         )
     spec = [load(sr_hbm, srv), load(si_hbm, siv)]
+    phase.wait()
+    row8 = lax.broadcasted_iota(jnp.int32, (8, 128), 0)
+    angle = jnp.zeros((8, 128), F32)
+    for f in range(4):
+        angle = jnp.where(lax.rem(row8, 4) == f, ph_ref[f], angle)
+    wv[...] = jnp.where(row8 < 4, jnp.cos(angle), jnp.sin(angle))
 
     rows = lax.broadcasted_iota(jnp.int32, (128, 128), 0)
     lanes = lax.broadcasted_iota(jnp.int32, (128, 128), 1)
@@ -304,32 +320,14 @@
         s = lax.rem(Y + d, GY)
         for part in range(2):
             remote(srv.at[0], al.at[part, s], a_ss.at[part, d], a_rs.at[part, s], X, s).wait_recv()
-        remote(pk_s, pk_l.at[1, s], pk_ss.at[1, d], pk_rs.at[1, s], X, s).wait_recv()
         remote(t_s.at[0], t_l.at[s], t_ss.at[d], t_rs.at[s], X, s).wait_recv()
-    for s in range(GY):
-        pl.when(has_xn)(remote(pk_s, pk_l.at[2, s], pk_ss.at[2, s], pk_rs.at[2, s], xn, Y).wait_recv)
-        pl.when(has_xp)(remote(pk_s, pk_l.at[0, s], pk_ss.at[0, s], pk_rs.at[0, s], xp, Y).wait_recv)
     for copy in tabs:
         copy.wait()
 
-    wave_cos = [jnp.cos(jnp.full((8, 128), ph_ref[f], F32))[0:1] for f in range(4)]
-    wave_sin = [jnp.sin(jnp.full((8, 128), ph_ref[f], F32))[0:1] for f in range(4)]
+    wave_cos, wave_sin = [wv[f : f + 1] for f in range(4)], [wv[f : f + 1] for f in range(4, 8)]
     total = None
     for s in range(GY):
-        nxt, own, prv = pk_l[2, s], pk_l[1, s], pk_l[0, s]
-        dhz = -0.5 * nxt[0:1]
-        before = -0.5 * pk_l[2, s - 1][0:1, 127:128] if s else jnp.zeros((1, 1), F32)
-        dhz_p = jnp.where(lane1 == 0, before, pltpu.roll(dhz, 1, 1))
-        dhy = 0.5 * nxt[1:2]
-        dhyd = dhy - 0.5 * nxt[2:3]
-        after = 0.5 * pk_l[0, s + 1][6:7, 0:1] if s < GY - 1 else jnp.zeros((1, 1), F32)
-        hzp = prv[3:4] - 0.5 * own[0:1] + jnp.where(lane1 == 127, after, 0.0)
-        last = jnp.where(
-            Y == 0, own[5:6] * (dhz - dhz_p - dhyd), jnp.where(Y == 1, -own[5:6] * dhz, jnp.where(Y == 3, dhy, 0.0))
-        )
-        head = jnp.where(jnp.logical_and(Y == 1, has_xp), own[4:5] * hzp, 0.0)
-        t = t_l[s, 0:16] + jnp.where(row16 == 15, last, 0.0) + jnp.where(row16 == 0, head, 0.0)
-        mine = t_l[s, 16:32]
+        t, mine = t_l[s, 0:16], t_l[s, 16:32]
         if s < GY - 1:
             after = t_l[s + 1, 16:32]
             exn, ez1n, ez0n, c127 = after[:, 0:1], after[:, 1:2], after[:, 2:3], mine[:, 5:6]
@@ -353,22 +351,56 @@
         total = part if total is None else total + part
     bs[...] = total.reshape(GX, 8, 128)
 
-    def column(d):
-        to = lax.rem(X + d, GX)
-        return remote(bs.at[to], bl.at[X], b_ss.at[d], b_rs.at[X], to, Y)
-
-    def b_start(d, carry):
-        column(d).start()
-        return carry
-
-    lax.fori_loop(1, GX, b_start, 0)
-
-    def b_sent(d, carry):
-        column(d).wait_send()
-        return carry
-
-    pending.append(lambda: lax.fori_loop(1, GX, b_sent, 0))
-    bl[X] = bs[X]
+    for d in range(1, GY):
+        s = lax.rem(Y + d, GY)
+        remote(pk_s, pk_l.at[1, s], pk_ss.at[1, d], pk_rs.at[1, s], X, s).wait_recv()
+    for s in range(GY):
+        pl.when(has_xn)(remote(pk_s, pk_l.at[2, s], pk_ss.at[2, s], pk_rs.at[2, s], xn, Y).wait_recv)
+        pl.when(has_xp)(remote(pk_s, pk_l.at[0, s], pk_ss.at[0, s], pk_rs.at[0, s], xp, Y).wait_recv)
+    added = None
+    none = jnp.zeros((1, 128), F32)
+    for s in range(GY):
+        nxt, own, prv = pk_l[2, s], pk_l[1, s], pk_l[0, s]
+        dhz = -0.5 * nxt[0:1]
+        before = -0.5 * pk_l[2, s - 1][0:1, 127:128] if s else jnp.zeros((1, 1), F32)
+        dhz_p = jnp.where(lane1 == 0, before, pltpu.roll(dhz, 1, 1))
+        dhy = 0.5 * nxt[1:2]
+        dhyd = dhy - 0.5 * nxt[2:3]
+        after = 0.5 * pk_l[0, s + 1][6:7, 0:1] if s < GY - 1 else jnp.zeros((1, 1), F32)
+        hzp = prv[3:4] - 0.5 * own[0:1] + jnp.where(lane1 == 127, after, 0.0)
+        last = jnp.where(
+            Y == 0, own[5:6] * (dhz - dhz_p - dhyd), jnp.where(Y == 1, -own[5:6] * dhz, jnp.where(Y == 3, dhy, 0.0))
+        )
+        head = jnp.where(jnp.logical_and(Y == 1, has_xp), own[4:5] * hzp, 0.0)
+        pair = [
+            jnp.where(row8 == 0, last, 0.0) + jnp.where(row8 == 1, head, 0.0),
+            jnp.where(row8 == 2, last, 0.0) + jnp.where(row8 == 3, head, 0.0),
+        ]
+        high, low = split(jnp.concatenate(pair, axis=1))
+        rhs = jnp.concatenate([high, low], axis=0)
+        part = dot_nt(ty[0, s], rhs) + dot_nt(ty[1, s], rhs)
+        added = part if added is None else added + part
+    added = added[:, 0:8] + added[:, 8:16]
+    wc, ws = none, none
+    for f in range(4):
+        wc = jnp.where((lane1 // 16) % 4 == f, wave_cos[f], wc)
+        ws = jnp.where((lane1 // 16) % 4 == f, wave_sin[f], ws)
+    by_cos, by_sin = jnp.where(lane1 < 64, wc, -ws), jnp.where(lane1 < 64, -ws, -wc)
+    is_last, is_head = lane1 % 16 == 15, lane1 % 16 == 0
+    extra = added[:, 0:1] * jnp.where(is_last, by_cos, 0.0) + added[:, 1:2] * jnp.where(is_head, by_cos, 0.0)
+    extra = extra + added[:, 2:3] * jnp.where(is_last, by_sin, 0.0) + added[:, 3:4] * jnp.where(is_head, by_sin, 0.0)
+    bs[...] = bs[...] + extra.reshape(GX, 8, 128)
+
+    x_hi, row_in = (X // 4) & 1, (X // 8) * 4 + (X & 3)
+
+    def column(at):
+        to = block_at(offsets[at])
+        return remote(bs.at[to], bl.at[x_hi, row_in], b_ss.at[at], b_rs.at[x_hi, row_in], to, Y)
+
+    for at in range(GX - 1):
+        column(at).start()
+        pending.append(column(at).wait_send)
+    bl[x_hi, row_in] = bs[X]
 
     def row(x, edge_first, edge_last):
         ex, ey, ez = eb[0, x], eb[1, x], eb[2, x]
@@ -422,20 +454,24 @@
     c = cb[0]
     eo[1, 0] = eo[1, 0] + c * hzp
     eo[2, 0] = eo[2, 0] - c * hyp
-    def b_wait(d, carry):
-        src = lax.rem(X + d, GX)
-        remote(bs.at[src], bl.at[src], b_ss.at[d], b_rs.at[src], src, Y).wait_recv()
-        return carry
-
-    lax.fori_loop(1, GX, b_wait, 0)
-
-    block = bl[...].reshape(256, 128)
-    sign = jnp.where(lax.broadcasted_iota(jnp.int32, (256, 128), 1) < 64, 1.0, -1.0)
-    both = jnp.concatenate([block, pltpu.roll(block, 64, 1) * sign], axis=0)
-    high, low = split(both)
-    y = dot_nn(tw[0], high) + dot_nn(tw[0], low) + dot_nn(tw[1], high)
+    def b_wait(o):
+        src = block_at(o)
+        at = ((src // 4) & 1, (src // 8) * 4 + (src & 3))
+        remote(bs.at[src], bl.at[at], b_ss.at[0], b_rs.at[at], src, Y).wait_recv()
+
+    sign = jnp.where(lax.broadcasted_iota(jnp.int32, (128, 128), 1) < 64, 1.0, -1.0)
+    y = None
+    for half in range(2):
+        for o in offsets[:-1]:
+            if o[1] == half:
+                b_wait(o)
+        which = (x_hi + half) & 1
+        block = bl[which].reshape(128, 128)
+        high, low = split(jnp.concatenate([block, pltpu.roll(block, 64, 1) * sign], axis=0))
+        part = dot_nn(tw[0, which], high) + dot_nn(tw[0, which], low) + dot_nn(tw[1, which], high)
+        y = part if y is None else y + part
     y = y * tt[0] + pltpu.roll(y, 64, 1) * tt[1]
-    y_sw = pltpu.roll(y, 64, 1) * sign
+    y_sw = pltpu.roll(y, 64, 1) * jnp.concatenate([sign, sign], axis=0)
     pieces = []
     for b in range(4):
         pieces += [y[64 * b : 64 * b + 64], y_sw[64 * b : 64 * b + 64]]
@@ -445,21 +481,15 @@
         for b in range(4):
             cs[4 * a + b] = out[4 * a : 4 * a + 4, 128 * b : 128 * b + 128]
 
-    def finished(d):
-        to = lax.rem(X + d, GX)
-        return remote(cs.at[to], cl.at[Y, slot], c_ss.at[d], c_rs.at[Y, slot], to, home)
-
-    def c_start(d, carry):
-        pl.when(jnp.logical_or(d > 0, home != Y))(finished(d).start)
-        return carry
-
-    lax.fori_loop(0, GX, c_start, 0)
-
-    def c_sent(d, carry):
-        pl.when(jnp.logical_or(d > 0, home != Y))(finished(d).wait_send)
-        return carry
-
-    pending.append(lambda: lax.fori_loop(0, GX, c_sent, 0))
+    def finished(at):
+        to = block_at(offsets[at])
+        return remote(cs.at[to], cl.at[Y, slot], c_ss.at[at], c_rs.at[Y, slot], to, home)
+
+    for at in range(GX - 1):
+        finished(at).start()
+        pending.append(finished(at).wait_send)
+    pl.when(home != Y)(finished(GX - 1).start)
+    pending.append(lambda: pl.when(home != Y)(finished(GX - 1).wait_send))
 
     @pl.when(home == Y)
     def _():
@@ -497,7 +527,11 @@
 
 
 def flush_kernel(eo, ho, nr, ni, rel, e_out, h_out, r_out, i_out, f_out, zz, fv, sem):
-    copies = [(eo.at[i], e_out.at[i]) for i in range(3)] + [(ho.at[i], h_out.at[i]) for i in range(3)]
+    copies = []
+    for i in range(3):
+        for x in range(0, 16, 4):
+            part = (i, pl.ds(x, 4))
+            copies += [(eo.at[part], e_out.at[part]), (ho.at[part], h_out.at[part])]
     copies += [(nr, r_out), (ni, i_out)]
     copies = [pltpu.make_async_copy(src, dst, sem.at[at]) for at, (src, dst) in enumerate(copies)]
     for copy in copies:
@@ -516,7 +550,7 @@
         for f in range(4):
             fv[0, g, f] = zz[4 * g + f, 0:8, 0:64]
             fv[1, g, f] = zz[4 * g + f, 8:16, 0:64]
-    copies.append(pltpu.make_async_copy(fv, f_out, sem.at[8]))
+    copies.append(pltpu.make_async_copy(fv, f_out, sem.at[26]))
     copies[-1].start()
     for copy in copies:
         copy.wait()
@@ -541,7 +575,7 @@
     held = pl.pallas_call(
         step_kernel,
         out_shape=shapes[:4] + [jax.ShapeDtypeStruct((8, 16, 128), F32)],
-        in_specs=[hbm] * 6 + [pl.BlockSpec(memory_space=pltpu.SMEM)] + [hbm] * 4,
+        in_specs=[hbm] * 11,
         out_specs=[in_vmem] * 5,
         scratch_shapes=[
             vmem(electric.shape, F32), vmem(magnetic.shape, F32), vmem(retention.shape, F32), vmem(coupling.shape, F32),
@@ -551,10 +585,10 @@
             vmem((2, 128, 128), F32), vmem((2, 128, 128), F32), vmem((8, 128), F32),
             vmem((8, 128), F32), vmem((3, 4, 8, 128), F32),
             vmem((4, 32, 128), F32), vmem((4, 32, 128), F32), vmem((2, 4, 4, 16, 128), F32),
-            vmem((32, 8, 128), F32), vmem((32, 8, 128), F32), vmem((32, 4, 128), F32), vmem((4, 8, 4, 128), F32),
-            vmem((2, 128, 128), F32), vmem((15, 16, 128), F32),
+            vmem((32, 8, 128), F32), vmem((2, 16, 8, 128), F32), vmem((32, 4, 128), F32), vmem((4, 8, 4, 128), F32),
+            vmem((2, 128, 128), F32), vmem((15, 16, 128), F32), vmem((8, 128), F32), pltpu.SMEM((4,), F32),
             dma((22,)), dma((4,)), dma((3, 4)), dma((3, 4)), dma((2, 4)), dma((2, 4)), dma((4,)), dma((4,)), dma((6,)),
-            dma((32,)), dma((32,)), dma((32,)), dma((4, 8)),
+            dma((32,)), dma((2, 16)), dma((32,)), dma((4, 8)), dma,
         ],
         compiler_params=pltpu.CompilerParams(collective_id=0, has_side_effects=True, vmem_limit_bytes=40 * 2**20),
     )(*fixed[:6], pltpu.with_memory_space_constraint(phases, pltpu.HBM), *fixed[6:])
@@ -563,7 +597,7 @@
         out_shape=shapes,
         in_specs=[in_vmem] * 5,
         out_specs=[hbm] * 5,
-        scratch_shapes=[vmem((16, 16, 128), F32), vmem((2, 4, 4, 8, 64), F32), dma((9,))],
+        scratch_shapes=[vmem((16, 16, 128), F32), vmem((2, 4, 4, 8, 64), F32), dma((27,))],
         compiler_params=pltpu.CompilerParams(vmem_limit_bytes=16 * 2**20),
     )(*held)
 

time: 39.6 us -> 37.9 us (0.957)
  Pallas kernels: 38.9 us -> 37.1 us
    pallas_call x1, Pallas kernels: 36 us -> 34.1 us  [per_device(): pl.pallas_call(step_kernel, out_shape=shapes[:4] + [jax.ShapeDtypeStruct(...]
where the time goes in v4:
time: 37.9 us; the launch traced here: 37.8 us
  Pallas kernels  37.1 us (98%)
  between operations  0.64 us (2%)
    pallas_call x1, Pallas kernels, per_device(): pl.pallas_call(step_kernel, out_shape=shapes[:4] + [jax.ShapeDtypeStruct(...  34.1 us
    pallas_call x1, Pallas kernels, per_device(): pl.pallas_call(flush_kernel, out_shape=shapes, in_specs=[in_vmem] * 5, ou...  3.08 us

profile of v4, /device:TPU:1, one launch (start us, length us, event | category | flops | bytes accessed | tf_op | source)
XLA Modules:
  0.0 37.8 jit_solution(16272005333174462020)
XLA Ops:
  0.6 34.1 %shard_map.146 = (f32[3,16,128,128]{3,2,1,0:T(8,128)S(1)}, f32[3,16,128,128]{3,2,1,0:T(8,128)S(1)}, f32[4,4,16,128]{3,2,1,0:T(8,128)S(1)}, f32[4,4,16,128]{3,2,1,0:T(8,128)S(1)}, f32[8,16,128]{2,1,0:T(8,128)S(1)}) custom-call(f32[3,16,128,128]{3,2,1,0:T(8,128)} %e_hbm.1, f32[3,16,128,128]{3,2,1,0:T(8,128)} %h_hbm.1, f32[16,128,128]{2,1,0:T(8,128)} %r_hbm.1, ...), custom_call_target="tpu_custom_call" | custom-call | tf_op jit(solution)/shard_map/pallas_call | solution.py:575
  34.7 3.1 %shard_map.147 = (f32[3,16,128,128]{3,2,1,0:T(8,128)}, f32[3,16,128,128]{3,2,1,0:T(8,128)}, f32[4,4,16,128]{3,2,1,0:T(8,128)}, f32[4,4,16,128]{3,2,1,0:T(8,128)}, f32[2,4,4,8,64]{4,3,2,1,0:T(8,128)}) custom-call(f32[3,16,128,128]{3,2,1,0:T(8,128)S(1)} %get-tuple-element.10.eo, f32[3,16,128,128]{3,2,1,0:T(8,128)S(1)} %get-tuple-element.11.ho, ...), custom_call_target="tpu_custom_call" | custom-call | tf_op jit(solution)/shard_map/pallas_call | solution.py:595

commit v5 on v4

--- a/solution.py
+++ b/solution.py
@@ -77,7 +77,7 @@
     eo, ho, nr, ni, rel,
     eb, hb, rb, cb, srv, siv, ty, tw, tt, tg,
     ye_s, yh_s, ye_l, yh_l, xe_l, xh_l, ce_l, pk_s, pk_l, t_s, t_l, al,
-    bs, bl, cs, cl, xh_s, pp, wv, ph_ref,
+    bs, bl, cs, cl, xh_s, pp, wv, ph_ref, gm, gt,
     ld_sem, yh_sem, pk_ss, pk_rs, a_ss, a_rs, t_ss, t_rs, x_sem, b_ss, b_rs, c_ss, c_rs, ph_sem,
 ):
     X = lax.axis_index("gx")
@@ -174,27 +174,32 @@
     def _():
         ce_l[...] = jnp.zeros_like(ce_l)
 
-    picks = (
-        (eb, 0, (110, 111, 112)), (eb, 1, (110, 111, 112)), (eb, 2, (110, 111)),
-        (hb, 0, (110, 111)), (hb, 1, (110, 111)), (hb, 2, (111,)),
-    )
-
-    def pick(x, carry):
-        at = 0
-        for ref, which, planes in picks:
-            v = ref[which, x]
-            for z in planes:
-                pp[at, pl.ds(x, 1), :] = plane_of(v, z)
-                at += 1
-        for ref in (rb, cb):
-            pp[at, pl.ds(x, 1), :] = plane_of(ref[x], PLANE)
-            at += 1
-        return carry
+    fields = [(eb, 0), (eb, 1), (eb, 2), (hb, 0), (hb, 1), (hb, 2), (rb, None), (cb, None)]
+    wanted = [(0, 0), (0, 1), (0, 2), (1, 0), (1, 1), (1, 2), (2, 0), (2, 1), (3, 0), (3, 1), (4, 0), (4, 1), (5, 1), (6, 1), (7, 1)]
+    lane32 = lax.broadcasted_iota(jnp.int32, (32, 128), 1)
+    window = jnp.logical_and(lane32 >= PLANE - 1, lane32 < PLANE + 3)
 
     for at in range(4):
         for copy in chunks[at]:
             copy.wait()
-        lax.fori_loop(4 * at, 4 * at + 4, pick, 0)
+
+        def gather(block, carry, at=at):
+            ys = pl.ds(pl.multiple_of(block * 32, 32), 32)
+            total = None
+            for which, (ref, comp) in enumerate(fields):
+                for x in range(4):
+                    v = ref[4 * at + x, ys, :] if comp is None else ref[comp, 4 * at + x, ys, :]
+                    v = jnp.where(window, v, 0.0)
+                    shift = (4 * (4 * which + x) - (PLANE - 1)) % 128
+                    v = pltpu.roll(v, shift, 1) if shift else v
+                    total = v if total is None else total + v
+            gm[ys, :] = total
+            return carry
+
+        lax.fori_loop(0, 4, gather, 0)
+        gt[...] = gm[...].T
+        for to, (which, z) in enumerate(wanted):
+            pp[to, 4 * at : 4 * at + 4, :] = gt[pl.ds(16 * which + z, 4, stride=4), :]
     tabs = [load(ty_hbm, ty), load(tw_hbm, tw), load(tt_hbm, tt), load(tg_hbm, tg)]
 
     ex0, ex1, ex2, ey0, ey1, ey2, ez0, ez1, hx0, hx1, hy0, hy1, hz1, r1, c1 = (pp[at] for at in range(15))
@@ -587,6 +592,7 @@
             vmem((4, 32, 128), F32), vmem((4, 32, 128), F32), vmem((2, 4, 4, 16, 128), F32),
             vmem((32, 8, 128), F32), vmem((2, 16, 8, 128), F32), vmem((32, 4, 128), F32), vmem((4, 8, 4, 128), F32),
             vmem((2, 128, 128), F32), vmem((15, 16, 128), F32), vmem((8, 128), F32), pltpu.SMEM((4,), F32),
+            vmem((128, 128), F32), vmem((128, 128), F32),
             dma((22,)), dma((4,)), dma((3, 4)), dma((3, 4)), dma((2, 4)), dma((2, 4)), dma((4,)), dma((4,)), dma((6,)),
             dma((32,)), dma((2, 16)), dma((32,)), dma((4, 8)), dma,
         ],

time: 37.9 us -> 36.2 us (0.955)
  Pallas kernels: 37.1 us -> 35.4 us
    pallas_call x1, Pallas kernels: 34.1 us -> 32.3 us  [per_device(): pl.pallas_call(step_kernel, out_shape=shapes[:4] + [jax.ShapeDtypeStruct(...]
where the time goes in v5:
time: 36.2 us; the launch traced here: 36 us
  Pallas kernels  35.4 us (98%)
  between operations  0.64 us (2%)
    pallas_call x1, Pallas kernels, per_device(): pl.pallas_call(step_kernel, out_shape=shapes[:4] + [jax.ShapeDtypeStruct(...  32.3 us
    pallas_call x1, Pallas kernels, per_device(): pl.pallas_call(flush_kernel, out_shape=shapes, in_specs=[in_vmem] * 5, ou...  3.08 us

profile of v5, /device:TPU:1, one launch (start us, length us, event | category | flops | bytes accessed | tf_op | source)
XLA Modules:
  0.0 36.0 jit_solution(5330789454669467425)
XLA Ops:
  0.6 32.3 %shard_map.146 = (f32[3,16,128,128]{3,2,1,0:T(8,128)S(1)}, f32[3,16,128,128]{3,2,1,0:T(8,128)S(1)}, f32[4,4,16,128]{3,2,1,0:T(8,128)S(1)}, f32[4,4,16,128]{3,2,1,0:T(8,128)S(1)}, f32[8,16,128]{2,1,0:T(8,128)S(1)}) custom-call(f32[3,16,128,128]{3,2,1,0:T(8,128)} %e_hbm.1, f32[3,16,128,128]{3,2,1,0:T(8,128)} %h_hbm.1, f32[16,128,128]{2,1,0:T(8,128)} %r_hbm.1, ...), custom_call_target="tpu_custom_call" | custom-call | tf_op jit(solution)/shard_map/pallas_call | solution.py:580
  33.0 3.1 %shard_map.147 = (f32[3,16,128,128]{3,2,1,0:T(8,128)}, f32[3,16,128,128]{3,2,1,0:T(8,128)}, f32[4,4,16,128]{3,2,1,0:T(8,128)}, f32[4,4,16,128]{3,2,1,0:T(8,128)}, f32[2,4,4,8,64]{4,3,2,1,0:T(8,128)}) custom-call(f32[3,16,128,128]{3,2,1,0:T(8,128)S(1)} %get-tuple-element.10.eo, f32[3,16,128,128]{3,2,1,0:T(8,128)S(1)} %get-tuple-element.11.ho, ...), custom_call_target="tpu_custom_call" | custom-call | tf_op jit(solution)/shard_map/pallas_call | solution.py:601

commit v6 on v5

--- a/solution.py
+++ b/solution.py
@@ -111,28 +111,21 @@
             greet(8 * Y + at_x[o[0]] + at_z[o[1]], y)
     greeted = 3 * (GY - 1) + (GX - 1) + jnp.where(home != Y, GX, 0)
 
-    loads = []
-
-    def load(src, dst):
-        copy = pltpu.make_async_copy(src, dst, ld_sem.at[len(loads)])
+    def load(src, dst, sem):
+        copy = pltpu.make_async_copy(src, dst, sem)
         copy.start()
-        loads.append(copy)
         return copy
 
     phase = pltpu.make_async_copy(ph_hbm, ph_ref, ph_sem)
     phase.start()
-    chunks = []
     for at in range(4):
         part = pl.ds(4 * at, 4)
-        chunks.append(
-            [
-                load(e_hbm.at[:, part], eb.at[:, part]),
-                load(h_hbm.at[:, part], hb.at[:, part]),
-                load(c_hbm.at[part], cb.at[part]),
-                load(r_hbm.at[part], rb.at[part]),
-            ]
-        )
-    spec = [load(sr_hbm, srv), load(si_hbm, siv)]
+        load(e_hbm.at[:, part], eb.at[:, part], ld_sem.at[at])
+        load(h_hbm.at[:, part], hb.at[:, part], ld_sem.at[at])
+        load(c_hbm.at[part], cb.at[part], ld_sem.at[at])
+        load(r_hbm.at[part], rb.at[part], ld_sem.at[at])
+    load(sr_hbm, srv, ld_sem.at[4])
+    load(si_hbm, siv, ld_sem.at[4])
     phase.wait()
     row8 = lax.broadcasted_iota(jnp.int32, (8, 128), 0)
     angle = jnp.zeros((8, 128), F32)
@@ -180,8 +173,7 @@
     window = jnp.logical_and(lane32 >= PLANE - 1, lane32 < PLANE + 3)
 
     for at in range(4):
-        for copy in chunks[at]:
-            copy.wait()
+        pltpu.make_async_copy(e_hbm.at[0:2], eb.at[0:2], ld_sem.at[at]).wait()
 
         def gather(block, carry, at=at):
             ys = pl.ds(pl.multiple_of(block * 32, 32), 32)
@@ -200,7 +192,8 @@
         gt[...] = gm[...].T
         for to, (which, z) in enumerate(wanted):
             pp[to, 4 * at : 4 * at + 4, :] = gt[pl.ds(16 * which + z, 4, stride=4), :]
-    tabs = [load(ty_hbm, ty), load(tw_hbm, tw), load(tt_hbm, tt), load(tg_hbm, tg)]
+    pairs = ((ty_hbm, ty), (tw_hbm, tw), (tt_hbm, tt), (tg_hbm, tg))
+    tabs = [load(src, dst, ld_sem.at[5 + at]) for at, (src, dst) in enumerate(pairs)]
 
     ex0, ex1, ex2, ey0, ey1, ey2, ez0, ez1, hx0, hx1, hy0, hy1, hz1, r1, c1 = (pp[at] for at in range(15))
 
@@ -241,8 +234,7 @@
     yh_s[1] = hb[2, :, 127, :] - 0.5 * (ey_up - ey + ex)
 
     pk_l[1, Y] = pk_s[...]
-    for copy in spec:
-        copy.wait()
+    pltpu.make_async_copy(c_hbm.at[0:4], cb.at[0:4], ld_sem.at[4]).wait()
     al[0, Y] = srv[Y]
     al[1, Y] = siv[Y]
     t_l[Y] = t_s[Y]
@@ -256,7 +248,7 @@
 
     def pack(dx, d):
         return remote(
-            pk_s, pk_l.at[2 - dx, Y], pk_ss.at[dx, d], pk_rs.at[2 - dx, Y], (xp, X, xn)[dx], lax.rem(Y + d, GY)
+            pk_s, pk_l.at[2 - dx, Y], pk_ss.at[dx], pk_rs.at[2 - dx], (xp, X, xn)[dx], lax.rem(Y + d, GY)
         )
 
     for dx, ok in ((0, has_xp), (2, has_xn)):
@@ -265,31 +257,32 @@
     for d in range(1, GY):
         pack(1, d).start()
 
+    def all_of(ref, ss, rs):
+        return remote(ref, ref, ss, rs, xp, Y)
+
     def packs_sent():
         for dx, ok in ((0, has_xp), (2, has_xn)):
-            for d in range(GY):
-                pl.when(ok)(pack(dx, d).wait_send)
-        for d in range(1, GY):
-            pack(1, d).wait_send()
+            pl.when(ok)(all_of(pk_l.at[0], pk_ss.at[dx], pk_rs.at[dx]).wait_send)
+        all_of(pk_l.at[0, 0:3], pk_ss.at[1], pk_rs.at[1]).wait_send()
 
     pending.append(packs_sent)
 
     def tangent(d):
         g = lax.rem(Y + d, GY)
-        return remote(t_s.at[g], t_l.at[Y], t_ss.at[d], t_rs.at[Y], X, g)
+        return remote(t_s.at[g], t_l.at[Y], t_ss, t_rs, X, g)
 
     for d in range(1, GY):
         tangent(d).start()
-        pending.append(tangent(d).wait_send)
+    pending.append(lambda: all_of(t_s.at[0:3], t_ss, t_rs).wait_send())
 
     def spectrum(part, d):
         g = lax.rem(Y + d, GY)
-        return remote((srv, siv)[part].at[g], al.at[part, Y], a_ss.at[part, d], a_rs.at[part, Y], X, g)
+        return remote((srv, siv)[part].at[g], al.at[part, Y], a_ss, a_rs, X, g)
 
     for d in range(1, GY):
         for part in range(2):
             spectrum(part, d).start()
-            pending.append(spectrum(part, d).wait_send)
+    pending.append(lambda: all_of(al.at[:, 0:3], a_ss, a_rs).wait_send())
 
     ye = remote(ye_s, ye_l, yh_sem.at[0], yh_sem.at[1], X, yp)
     yh = remote(yh_s, yh_l, yh_sem.at[2], yh_sem.at[3], X, yn)
@@ -321,11 +314,8 @@
     def from_gy(make, d):
         make(d).wait_recv()
 
-    for d in range(1, GY):
-        s = lax.rem(Y + d, GY)
-        for part in range(2):
-            remote(srv.at[0], al.at[part, s], a_ss.at[part, d], a_rs.at[part, s], X, s).wait_recv()
-        remote(t_s.at[0], t_l.at[s], t_ss.at[d], t_rs.at[s], X, s).wait_recv()
+    all_of(al.at[:, 0:3], a_ss, a_rs).wait_recv()
+    all_of(t_l.at[0:3], t_ss, t_rs).wait_recv()
     for copy in tabs:
         copy.wait()
 
@@ -356,12 +346,9 @@
         total = part if total is None else total + part
     bs[...] = total.reshape(GX, 8, 128)
 
-    for d in range(1, GY):
-        s = lax.rem(Y + d, GY)
-        remote(pk_s, pk_l.at[1, s], pk_ss.at[1, d], pk_rs.at[1, s], X, s).wait_recv()
-    for s in range(GY):
-        pl.when(has_xn)(remote(pk_s, pk_l.at[2, s], pk_ss.at[2, s], pk_rs.at[2, s], xn, Y).wait_recv)
-        pl.when(has_xp)(remote(pk_s, pk_l.at[0, s], pk_ss.at[0, s], pk_rs.at[0, s], xp, Y).wait_recv)
+    all_of(pk_l.at[1, 0:3], pk_ss.at[1], pk_rs.at[1]).wait_recv()
+    pl.when(has_xn)(all_of(pk_l.at[2], pk_ss.at[2], pk_rs.at[2]).wait_recv)
+    pl.when(has_xp)(all_of(pk_l.at[0], pk_ss.at[0], pk_rs.at[0]).wait_recv)
     added = None
     none = jnp.zeros((1, 128), F32)
     for s in range(GY):
@@ -400,11 +387,11 @@
 
     def column(at):
         to = block_at(offsets[at])
-        return remote(bs.at[to], bl.at[x_hi, row_in], b_ss.at[at], b_rs.at[x_hi, row_in], to, Y)
+        return remote(bs.at[to], bl.at[x_hi, row_in], b_ss, b_rs.at[offsets[at][1]], to, Y)
 
     for at in range(GX - 1):
         column(at).start()
-        pending.append(column(at).wait_send)
+    pending.append(lambda: all_of(bs.at[0:31], b_ss, b_rs.at[0]).wait_send())
     bl[x_hi, row_in] = bs[X]
 
     def row(x, edge_first, edge_last):
@@ -443,6 +430,44 @@
     lax.fori_loop(1, 15, inner, 0)
     row(15, False, True)
 
+    sign = jnp.where(lax.broadcasted_iota(jnp.int32, (128, 128), 1) < 64, 1.0, -1.0)
+    y = None
+    for half in range(2):
+        all_of(bs.at[0 : 15 + half], b_ss, b_rs.at[half]).wait_recv()
+        which = (x_hi + half) & 1
+        block = bl[which].reshape(128, 128)
+        high, low = split(jnp.concatenate([block, pltpu.roll(block, 64, 1) * sign], axis=0))
+        part = dot_nn(tw[0, which], high) + dot_nn(tw[0, which], low) + dot_nn(tw[1, which], high)
+        y = part if y is None else y + part
+    y = y * tt[0] + pltpu.roll(y, 64, 1) * tt[1]
+    y_sw = pltpu.roll(y, 64, 1) * jnp.concatenate([sign, sign], axis=0)
+    pieces = []
+    for b in range(4):
+        pieces += [y[64 * b : 64 * b + 64], y_sw[64 * b : 64 * b + 64]]
+    high, low = split(jnp.concatenate(pieces, axis=0))
+    out = dot_nt(tg[0], high) + dot_nt(tg[0], low) + dot_nt(tg[1], high)
+    for a in range(8):
+        for b in range(4):
+            cs[4 * a + b] = out[4 * a : 4 * a + 4, 128 * b : 128 * b + 128]
+
+    def finished(at):
+        to = block_at(offsets[at])
+        return remote(cs.at[to], cl.at[Y, slot], c_ss, c_rs, to, home)
+
+    for at in range(GX - 1):
+        finished(at).start()
+    pl.when(home != Y)(finished(GX - 1).start)
+
+    def blocks(wait):
+        pl.when(home != Y)(lambda: wait(all_of(cs, c_ss, c_rs)))
+        pl.when(home == Y)(lambda: wait(all_of(cs.at[0:31], c_ss, c_rs)))
+
+    pending.append(lambda: blocks(lambda copy: copy.wait_send()))
+
+    @pl.when(home == Y)
+    def _():
+        cl[Y, slot] = cs[X]
+
     pl.when(has_xn)(xe.wait_recv)
     pl.when(has_xp)(xh.wait_recv)
     pl.when(jnp.logical_and(has_xn, has_yp))(corner.wait_recv)
@@ -459,46 +484,6 @@
     c = cb[0]
     eo[1, 0] = eo[1, 0] + c * hzp
     eo[2, 0] = eo[2, 0] - c * hyp
-    def b_wait(o):
-        src = block_at(o)
-        at = ((src // 4) & 1, (src // 8) * 4 + (src & 3))
-        remote(bs.at[src], bl.at[at], b_ss.at[0], b_rs.at[at], src, Y).wait_recv()
-
-    sign = jnp.where(lax.broadcasted_iota(jnp.int32, (128, 128), 1) < 64, 1.0, -1.0)
-    y = None
-    for half in range(2):
-        for o in offsets[:-1]:
-            if o[1] == half:
-                b_wait(o)
-        which = (x_hi + half) & 1
-        block = bl[which].reshape(128, 128)
-        high, low = split(jnp.concatenate([block, pltpu.roll(block, 64, 1) * sign], axis=0))
-        part = dot_nn(tw[0, which], high) + dot_nn(tw[0, which], low) + dot_nn(tw[1, which], high)
-        y = part if y is None else y + part
-    y = y * tt[0] + pltpu.roll(y, 64, 1) * tt[1]
-    y_sw = pltpu.roll(y, 64, 1) * jnp.concatenate([sign, sign], axis=0)
-    pieces = []
-    for b in range(4):
-        pieces += [y[64 * b : 64 * b + 64], y_sw[64 * b : 64 * b + 64]]
-    high, low = split(jnp.concatenate(pieces, axis=0))
-    out = dot_nt(tg[0], high) + dot_nt(tg[0], low) + dot_nt(tg[1], high)
-    for a in range(8):
-        for b in range(4):
-            cs[4 * a + b] = out[4 * a : 4 * a + 4, 128 * b : 128 * b + 128]
-
-    def finished(at):
-        to = block_at(offsets[at])
-        return remote(cs.at[to], cl.at[Y, slot], c_ss.at[at], c_rs.at[Y, slot], to, home)
-
-    for at in range(GX - 1):
-        finished(at).start()
-        pending.append(finished(at).wait_send)
-    pl.when(home != Y)(finished(GX - 1).start)
-    pending.append(lambda: pl.when(home != Y)(finished(GX - 1).wait_send))
-
-    @pl.when(home == Y)
-    def _():
-        cl[Y, slot] = cs[X]
 
     def own_plane(x, carry):
         for at, v in enumerate((eo[0, x], eo[1, x], ho[0, x], ho[1, x])):
@@ -512,17 +497,7 @@
             nr[at, f] = srv[at, f] + t * wave_cos[f]
             ni[at, f] = siv[at, f] - t * wave_sin[f]
 
-    def c_wait(i, carry):
-        g, q = i // 8, lax.rem(i, 8)
-        src = 8 * Y + q
-
-        @pl.when(jnp.logical_or(g != Y, src != X))
-        def _():
-            remote(cs.at[0], cl.at[g, q], c_ss.at[0], c_rs.at[g, q], src, g).wait_recv()
-
-        return carry
-
-    lax.fori_loop(0, 32, c_wait, 0)
+    blocks(lambda copy: copy.wait_recv())
 
     for q in range(8):
         for g in range(4):
@@ -532,13 +507,13 @@
 
 
 def flush_kernel(eo, ho, nr, ni, rel, e_out, h_out, r_out, i_out, f_out, zz, fv, sem):
-    copies = []
-    for i in range(3):
-        for x in range(0, 16, 4):
-            part = (i, pl.ds(x, 4))
-            copies += [(eo.at[part], e_out.at[part]), (ho.at[part], h_out.at[part])]
-    copies += [(nr, r_out), (ni, i_out)]
-    copies = [pltpu.make_async_copy(src, dst, sem.at[at]) for at, (src, dst) in enumerate(copies)]
+    for which, (src, dst) in enumerate(((eo, e_out), (ho, h_out))):
+        for i in range(3):
+            for x in range(0, 16, 8):
+                part = (i, pl.ds(x, 8))
+                pltpu.make_async_copy(src.at[part], dst.at[part], sem.at[which]).start()
+    whole = [pltpu.make_async_copy(src, dst, sem.at[at]) for at, (src, dst) in enumerate(((eo, e_out), (ho, h_out)))]
+    copies = [pltpu.make_async_copy(nr, r_out, sem.at[2]), pltpu.make_async_copy(ni, i_out, sem.at[3])]
     for copy in copies:
         copy.start()
     lane16 = lax.broadcasted_iota(jnp.int32, (16, 128), 1)
@@ -555,9 +530,9 @@
         for f in range(4):
             fv[0, g, f] = zz[4 * g + f, 0:8, 0:64]
             fv[1, g, f] = zz[4 * g + f, 8:16, 0:64]
-    copies.append(pltpu.make_async_copy(fv, f_out, sem.at[26]))
+    copies.append(pltpu.make_async_copy(fv, f_out, sem.at[4]))
     copies[-1].start()
-    for copy in copies:
+    for copy in copies + whole:
         copy.wait()
 
 
@@ -593,8 +568,7 @@
             vmem((32, 8, 128), F32), vmem((2, 16, 8, 128), F32), vmem((32, 4, 128), F32), vmem((4, 8, 4, 128), F32),
             vmem((2, 128, 128), F32), vmem((15, 16, 128), F32), vmem((8, 128), F32), pltpu.SMEM((4,), F32),
             vmem((128, 128), F32), vmem((128, 128), F32),
-            dma((22,)), dma((4,)), dma((3, 4)), dma((3, 4)), dma((2, 4)), dma((2, 4)), dma((4,)), dma((4,)), dma((6,)),
-            dma((32,)), dma((2, 16)), dma((32,)), dma((4, 8)), dma,
+            dma((9,)), dma((4,)), dma((3,)), dma((3,)), dma, dma, dma, dma, dma((6,)), dma, dma((2,)), dma, dma, dma,
         ],
         compiler_params=pltpu.CompilerParams(collective_id=0, has_side_effects=True, vmem_limit_bytes=40 * 2**20),
     )(*fixed[:6], pltpu.with_memory_space_constraint(phases, pltpu.HBM), *fixed[6:])
@@ -603,7 +577,7 @@
         out_shape=shapes,
         in_specs=[in_vmem] * 5,
         out_specs=[hbm] * 5,
-        scratch_shapes=[vmem((16, 16, 128), F32), vmem((2, 4, 4, 8, 64), F32), dma((27,))],
+        scratch_shapes=[vmem((16, 16, 128), F32), vmem((2, 4, 4, 8, 64), F32), dma((5,))],
         compiler_params=pltpu.CompilerParams(vmem_limit_bytes=16 * 2**20),
     )(*held)
 

time: 36.2 us -> 34.1 us (0.942)
  Pallas kernels: 35.4 us -> 33.4 us
    pallas_call x1, Pallas kernels: 32.3 us -> 30.5 us  [per_device(): pl.pallas_call(step_kernel, out_shape=shapes[:4] + [jax.ShapeDtypeStruct(...]
where the time goes in v6:
time: 34.1 us; the launch traced here: 34 us
  Pallas kernels  33.4 us (98%)
  between operations  0.64 us (2%)
    pallas_call x1, Pallas kernels, per_device(): pl.pallas_call(step_kernel, out_shape=shapes[:4] + [jax.ShapeDtypeStruct(...  30.5 us
    pallas_call x1, Pallas kernels, per_device(): pl.pallas_call(flush_kernel, out_shape=shapes, in_specs=[in_vmem] * 5, ou...  2.89 us

profile of v6, /device:TPU:1, one launch (start us, length us, event | category | flops | bytes accessed | tf_op | source)
XLA Modules:
  0.0 34.0 jit_solution(10492357374593346997)
XLA Ops:
  0.6 30.5 %shard_map.146 = (f32[3,16,128,128]{3,2,1,0:T(8,128)S(1)}, f32[3,16,128,128]{3,2,1,0:T(8,128)S(1)}, f32[4,4,16,128]{3,2,1,0:T(8,128)S(1)}, f32[4,4,16,128]{3,2,1,0:T(8,128)S(1)}, f32[8,16,128]{2,1,0:T(8,128)S(1)}) custom-call(f32[3,16,128,128]{3,2,1,0:T(8,128)} %e_hbm.1, f32[3,16,128,128]{3,2,1,0:T(8,128)} %h_hbm.1, f32[16,128,128]{2,1,0:T(8,128)} %r_hbm.1, ...), custom_call_target="tpu_custom_call" | custom-call | tf_op jit(solution)/shard_map/pallas_call | solution.py:555
  31.1 2.9 %shard_map.147 = (f32[3,16,128,128]{3,2,1,0:T(8,128)}, f32[3,16,128,128]{3,2,1,0:T(8,128)}, f32[4,4,16,128]{3,2,1,0:T(8,128)}, f32[4,4,16,128]{3,2,1,0:T(8,128)}, f32[2,4,4,8,64]{4,3,2,1,0:T(8,128)}) custom-call(f32[3,16,128,128]{3,2,1,0:T(8,128)S(1)} %get-tuple-element.10.eo, f32[3,16,128,128]{3,2,1,0:T(8,128)S(1)} %get-tuple-element.11.ho, ...), custom_call_target="tpu_custom_call" | custom-call | tf_op jit(solution)/shard_map/pallas_call | solution.py:575

commit v7 on v6

--- a/solution.py
+++ b/solution.py
@@ -346,11 +346,19 @@
         total = part if total is None else total + part
     bs[...] = total.reshape(GX, 8, 128)
 
+    none = jnp.zeros((1, 128), F32)
+    wc, ws = none, none
+    for f in range(4):
+        wc = jnp.where((lane1 // 16) % 4 == f, wave_cos[f], wc)
+        ws = jnp.where((lane1 // 16) % 4 == f, wave_sin[f], ws)
+    by_cos, by_sin = jnp.where(lane1 < 64, wc, -ws), jnp.where(lane1 < 64, -ws, -wc)
+    is_last, is_head = lane1 % 16 == 15, lane1 % 16 == 0
+    cos_last, cos_head = jnp.where(is_last, by_cos, 0.0), jnp.where(is_head, by_cos, 0.0)
+    sin_last, sin_head = jnp.where(is_last, by_sin, 0.0), jnp.where(is_head, by_sin, 0.0)
     all_of(pk_l.at[1, 0:3], pk_ss.at[1], pk_rs.at[1]).wait_recv()
     pl.when(has_xn)(all_of(pk_l.at[2], pk_ss.at[2], pk_rs.at[2]).wait_recv)
     pl.when(has_xp)(all_of(pk_l.at[0], pk_ss.at[0], pk_rs.at[0]).wait_recv)
     added = None
-    none = jnp.zeros((1, 128), F32)
     for s in range(GY):
         nxt, own, prv = pk_l[2, s], pk_l[1, s], pk_l[0, s]
         dhz = -0.5 * nxt[0:1]
@@ -373,14 +381,7 @@
         part = dot_nt(ty[0, s], rhs) + dot_nt(ty[1, s], rhs)
         added = part if added is None else added + part
     added = added[:, 0:8] + added[:, 8:16]
-    wc, ws = none, none
-    for f in range(4):
-        wc = jnp.where((lane1 // 16) % 4 == f, wave_cos[f], wc)
-        ws = jnp.where((lane1 // 16) % 4 == f, wave_sin[f], ws)
-    by_cos, by_sin = jnp.where(lane1 < 64, wc, -ws), jnp.where(lane1 < 64, -ws, -wc)
-    is_last, is_head = lane1 % 16 == 15, lane1 % 16 == 0
-    extra = added[:, 0:1] * jnp.where(is_last, by_cos, 0.0) + added[:, 1:2] * jnp.where(is_head, by_cos, 0.0)
-    extra = extra + added[:, 2:3] * jnp.where(is_last, by_sin, 0.0) + added[:, 3:4] * jnp.where(is_head, by_sin, 0.0)
+    extra = added[:, 0:1] * cos_last + added[:, 1:2] * cos_head + added[:, 2:3] * sin_last + added[:, 3:4] * sin_head
     bs[...] = bs[...] + extra.reshape(GX, 8, 128)
 
     x_hi, row_in = (X // 4) & 1, (X // 8) * 4 + (X & 3)

time: 34.1 us -> 34.1 us (level)
  no operation moved by 1% of the time
where the time goes in v7:
time: 34.1 us; the launch traced here: 34 us
  Pallas kernels  33.4 us (98%)
  between operations  0.64 us (2%)
    pallas_call x1, Pallas kernels, per_device(): pl.pallas_call(step_kernel, out_shape=shapes[:4] + [jax.ShapeDtypeStruct(...  30.5 us
    pallas_call x1, Pallas kernels, per_device(): pl.pallas_call(flush_kernel, out_shape=shapes, in_specs=[in_vmem] * 5, ou...  2.89 us

profile of v7, /device:TPU:1, one launch (start us, length us, event | category | flops | bytes accessed | tf_op | source)
XLA Modules:
  0.0 34.0 jit_solution(13227234257560827469)
XLA Ops:
  0.6 30.5 %shard_map.146 = (f32[3,16,128,128]{3,2,1,0:T(8,128)S(1)}, f32[3,16,128,128]{3,2,1,0:T(8,128)S(1)}, f32[4,4,16,128]{3,2,1,0:T(8,128)S(1)}, f32[4,4,16,128]{3,2,1,0:T(8,128)S(1)}, f32[8,16,128]{2,1,0:T(8,128)S(1)}) custom-call(f32[3,16,128,128]{3,2,1,0:T(8,128)} %e_hbm.1, f32[3,16,128,128]{3,2,1,0:T(8,128)} %h_hbm.1, f32[16,128,128]{2,1,0:T(8,128)} %r_hbm.1, ...), custom_call_target="tpu_custom_call" | custom-call | tf_op jit(solution)/shard_map/pallas_call | solution.py:556
  31.1 2.9 %shard_map.147 = (f32[3,16,128,128]{3,2,1,0:T(8,128)}, f32[3,16,128,128]{3,2,1,0:T(8,128)}, f32[4,4,16,128]{3,2,1,0:T(8,128)}, f32[4,4,16,128]{3,2,1,0:T(8,128)}, f32[2,4,4,8,64]{4,3,2,1,0:T(8,128)}) custom-call(f32[3,16,128,128]{3,2,1,0:T(8,128)S(1)} %get-tuple-element.10.eo, f32[3,16,128,128]{3,2,1,0:T(8,128)S(1)} %get-tuple-element.11.ho, ...), custom_call_target="tpu_custom_call" | custom-call | tf_op jit(solution)/shard_map/pallas_call | solution.py:576
